TPU v7x, 256 devices: a whole 4x4x8 slice. The times are simulated.
256 devices in a mesh: px: 32 (over y, z_hi, core), py: 8 (over z_lo, x).
Axes of the slice: x: 4, y: 4, z: 8 (z_hi: 4, z_lo: 2; z = z_hi * 2 + z_lo), core: 2. Of those that a mesh axis runs over, the one named last changes fastest.
Arguments:
- charges_old: float32 [32, 8, 32, 32, 512], P('px', 'py'), may hold values from -0.0026758191 to 0.0026758191
- spline_moduli: float32 [3, 512], replicated, may hold values from 1 to 2.5
Outputs:
- structure: float32 [2, 512, 512, 512], P(None, 'px', 'py')
- energy: float32 [], replicated
- virial: float32 [6], replicated
All inputs are finite; a program needn't handle non-finite values.
Results may differ from a plain program's by a relative error of at most 0.0007.
Values sent between devices are 32-bit elements; how exact they have to be, the bound alone decides.
No kernel may reach another device: no remote copies, remote signals or barrier semaphores. Data moves between devices by JAX's collectives and lax.ppermute only.
A program may use at most 128 MiB of HBM per device.

v0:
```python
import math

import jax
import jax.numpy as jnp
import numpy as np
from jax import lax
from jax.experimental import pallas as pl
from jax.experimental.pallas import tpu as pltpu
from jax.sharding import Mesh
from jax.sharding import PartitionSpec as P

PX = ("px_0", "px_1", "px_2")
PY = ("py_0", "py_1")
ALL = ("px_0", "px_1", "px_2", "py_0", "py_1")
FIRST = ("px_2", "py_0", "py_1")

GRID = 512
beta_nm = 3.12
cell_nm = 0.1
RATE = math.pi**2 / beta_nm**2
VOLUME = (cell_nm * GRID) ** 3
ROWS_A = 10
ROWS_B = 6
STEP = 2
EXT = 264
f32 = jnp.float32
bf16 = jnp.bfloat16


def split_table(table):
    high = table.astype(bf16)
    low = (table - high.astype(np.float64)).astype(bf16)
    return high, low


def z_table():
    z = np.arange(GRID)[:, None]
    column = np.arange(GRID)[None, :]
    kz = column // 64 * 32 + column % 32
    part = column // 32 % 2
    lane = np.arange(128)[None, :]
    kz = np.concatenate([kz, (lane % 8 + 1) * 32], axis=1)
    part = np.concatenate([part, lane // 32 % 2], axis=1)
    angle = z * kz % GRID * (2.0 * np.pi / GRID)
    return split_table(np.where(part == 0, np.cos(angle), -np.sin(angle)))


def circle(turns):
    angle = turns % GRID * (2.0 * np.pi / GRID)
    return np.cos(angle).astype(np.float32), np.sin(angle).astype(np.float32)


def y_factors():
    y = np.arange(256)[None, :]
    return *circle(16 * np.arange(32)[:, None] * y), *circle(np.arange(16)[:, None] * y)


def x_factors():
    kx = np.arange(256)[None, :]
    return *circle(32 * np.arange(16)[:, None] * kx), *circle(np.r_[0:32:2, 1:32:2][:, None] * kx)


def wave_rows():
    index = np.arange(GRID)
    back = (GRID - index) % GRID
    wave = (index - GRID * (index >= GRID // 2)) / (cell_nm * GRID)
    rows = [wave, wave * wave, np.exp(-RATE * wave * wave), wave[back]]
    return np.stack(rows).astype(np.float32)


def halves(value):
    high = value.astype(bf16)
    return high, (value - high.astype(f32)).astype(bf16)


def dot(a, b):
    return jnp.dot(a, b, preferred_element_type=f32)


def lane_index(shape):
    return lax.broadcasted_iota(jnp.int32, shape, len(shape) - 1)


def z_kernel(x_ref, high_ref, low_ref, out_ref, ext_ref):
    step = pl.program_id(0)
    core = step // 2
    x_high, x_low = halves(x_ref[...].reshape(256, GRID))
    w_high = high_ref[...]
    result = dot(x_high, w_high) + dot(x_low, w_high) + dot(x_high, low_ref[...])
    low_lanes = lane_index((32, 128)) < 64
    lane = lane_index((8, 128))
    for k in range(4):
        row = pl.multiple_of((step % 2) * 128 + k * 32, 32)
        even = result[k * 64 : k * 64 + 32]
        odd = result[k * 64 + 32 : k * 64 + 64]
        for t in range(4):
            e = even[:, t * 128 : t * 128 + 128]
            o = odd[:, t * 128 : t * 128 + 128]
            first = jnp.where(low_lanes, e, pltpu.roll(o, 64, 1))
            second = jnp.where(low_lanes, pltpu.roll(e, 64, 1), o)
            out_ref[core * 8 + t, pl.ds(row, 32), :] = first
            out_ref[core * 8 + 7 - t, pl.ds(row, 32), :] = second
        extra = jnp.zeros((8, 128), f32)
        for parity in range(2):
            for quarter in range(4):
                start = k * 64 + parity * 32 + quarter * 8
                piece = result[start : start + 8, 512:]
                here = (lane // 64 == parity) & (lane // 8 % 4 == quarter)
                extra = jnp.where(here, piece, extra)
        ext_ref[step * 4 + k] = extra

    @pl.when(step == 3)
    def _():
        for c in range(2):
            for h in range(8):
                packed = jnp.zeros((8, 128), f32)
                for x in range(8):
                    moved = pltpu.roll(ext_ref[c * 8 + x], (x - h) % 128, 1)
                    packed = jnp.where(lane % 8 == x, moved, packed)
                out_ref[c * 8 + (7 - h // 2 if h % 2 else h // 2), 256:EXT, :] = packed


def z_stage(block, tables):
    return pl.pallas_call(
        z_kernel,
        grid=(4,),
        in_specs=[
            pl.BlockSpec((8, 32, GRID), lambda i: (i, 0, 0)),
            pl.BlockSpec((GRID, 640), lambda i: (0, 0)),
            pl.BlockSpec((GRID, 640), lambda i: (0, 0)),
        ],
        out_specs=pl.BlockSpec((16, EXT, 128), lambda i: (0, 0, 0)),
        out_shape=jax.ShapeDtypeStruct((16, EXT, 128), f32),
        scratch_shapes=[pltpu.VMEM((16, 8, 128), f32)],
        name="z_stage",
        cost_estimate=pl.CostEstimate(flops=4 * 10**9, bytes_accessed=6 * 10**6, transcendentals=0),
    )(block, *tables)


def y_kernel(offsets, g_ref, pc_ref, ps_ref, oc_ref, os_ref, out_ref):
    rows = len(offsets)
    lane = lane_index((32, 128))
    real = lane // 32 % 2 == 0
    back = lane // 32 * 32 + (32 - lane % 32) % 32
    slot = lane % 32 == 0
    groups = [[o for o in offsets if o % 2 == parity] for parity in range(2)]
    pc = pc_ref[...]
    ps = ps_ref[...]
    tables = []
    for group in groups:
        cosines = [pc * oc_ref[o : o + 1, :] - ps * os_ref[o : o + 1, :] for o in group]
        sines = [ps * oc_ref[o : o + 1, :] + pc * os_ref[o : o + 1, :] for o in group]
        tables.append(halves(jnp.concatenate(cosines + sines, axis=0)))

    def products(low, high):
        results = []
        for (t_high, t_low), g in zip(tables, (low + high, low - high)):
            g_high, g_low = halves(g)
            results.append(dot(t_high, g_high) + dot(t_low, g_high) + dot(t_high, g_low))
        return results

    def pieces(results, columns):
        for parity, group in enumerate(groups):
            count = len(group) * 32
            for k, o in enumerate(group):
                p = results[parity][k * 32 : k * 32 + 32, columns]
                q = results[parity][count + k * 32 : count + k * 32 + 32, columns]
                turned = jnp.where(real, pltpu.roll(q, 96, 1), -pltpu.roll(q, 32, 1))
                other = p - turned
                yield offsets.index(o), p + turned, jnp.where(real, other, -other)

    def unpacked(start):
        parts = []
        for s in range(start, start + 8):
            packed = g_ref[s, 256:EXT, :]
            for quarter in range(4):
                parts.append(pltpu.roll(packed, 128 - 8 * quarter, 1) if quarter else packed)
        return jnp.concatenate(parts, axis=0)

    extra = {k: m for k, _, m in pieces(products(unpacked(0), unpacked(8)), slice(0, 128))}

    for pair in range(4):
        sides = []
        for start in (0, 8):
            columns = [
                g_ref[start : start + 8, x2 * 32 : x2 * 32 + 32, :].reshape(256, 128)
                for x2 in (2 * pair, 2 * pair + 1)
            ]
            sides.append(jnp.concatenate(columns, axis=1))
        results = products(*sides)
        for x2 in (2 * pair, 2 * pair + 1):
            first = x2 % 2 * 128
            for k, direct, mirror in pieces(results, slice(first, first + 128)):
                moved = pltpu.roll(extra[k], 128 - x2, 1) if x2 else extra[k]
                mirror = jnp.where(slot, moved, mirror)
                mirror = jnp.take_along_axis(mirror, back, axis=1)
                stride = 2 * rows * 8
                out_ref[pl.ds(k * 8 + x2, 32, stride=stride), :] = direct
                out_ref[pl.ds((rows + k) * 8 + x2, 32, stride=stride), :] = mirror


def x_table_rows(ac_ref, as_ref, bc_ref, bs_ref, high_ref, low_ref):
    for parity in range(2):
        bc = bc_ref[parity * 16 : parity * 16 + 16, :]
        bs = bs_ref[parity * 16 : parity * 16 + 16, :]
        for a in range(16):
            ac = ac_ref[a : a + 1, :]
            sa = as_ref[a : a + 1, :]
            full = jnp.concatenate([ac * bc - sa * bs, sa * bc + ac * bs], axis=1)
            high, low = halves(full)
            high_ref[parity, a * 16 : a * 16 + 16, :] = high
            low_ref[parity, a * 16 : a * 16 + 16, :] = low


def y_stage(blocks, offsets, with_tables):
    offsets = list(offsets)
    rows = len(offsets)

    def kernel(*refs):
        if with_tables:
            y_kernel(offsets, *refs[:5], refs[9])
            x_table_rows(*refs[5:9], *refs[10:])
        else:
            y_kernel(offsets, *refs)

    inputs = [blocks, *y_factors()]
    out_shape = [jax.ShapeDtypeStruct((64 * rows * 8, 128), f32)]
    if with_tables:
        inputs += x_factors()
        out_shape += [jax.ShapeDtypeStruct((2, 256, GRID), bf16)] * 2
    whole = pl.BlockSpec(memory_space=pltpu.VMEM)
    return pl.pallas_call(
        kernel,
        in_specs=[whole] * len(inputs),
        out_specs=[whole] * len(out_shape),
        out_shape=out_shape,
        name=f"y_stage_{rows}",
        cost_estimate=pl.CostEstimate(flops=4 * 10**9, bytes_accessed=6 * 10**6, transcendentals=0),
    )(*inputs)


def x_planes(high, g_ref, high_ref, low_ref, out_ref):
    turned = {}
    for o in range(STEP):
        for s in range(2):
            block = g_ref[:, s, o * 8 : o * 8 + 8, :].reshape(256, 128)
            turned[o, s] = jnp.transpose(block)
    half = STEP * 64
    real = []
    imag = []
    for parity in range(2):
        rows = [
            turned[o, s][parity * 64 + part * 32 : parity * 64 + part * 32 + 32]
            for part in range(2)
            for o in range(STEP)
            for s in range(2)
        ]
        a_high, a_low = halves(jnp.concatenate(rows, axis=0))
        w_high = high_ref[parity]
        result = dot(a_high, w_high) + dot(a_low, w_high) + dot(a_high, low_ref[parity])
        real.append(result[:half, :256] + result[half:, 256:])
        imag.append(result[half:, :256] - result[:half, 256:])
    full_real = jnp.concatenate([real[0] + real[1], real[0] - real[1]], axis=1)
    full_imag = jnp.concatenate([imag[0] + imag[1], imag[0] - imag[1]], axis=1)
    for o in range(STEP):
        for s in range(2):
            base = pl.multiple_of(32 * jnp.bitwise_xor(high, s), 32)
            start = o * 64 + s * 32
            out_ref[0, o, pl.ds(base, 32), :] = full_real[start : start + 32]
            out_ref[1, o, pl.ds(base, 32), :] = full_imag[start : start + 32]


def fold(value):
    return value.reshape(8, 8, GRID).sum(axis=0)


def x_kernel_a(side_ref, y_ref, g_ref, high_ref, low_ref, row_ref, col_ref, out_ref, sum_ref, acc_ref):
    step = pl.program_id(0)
    x_planes(side_ref[0], g_ref, high_ref, low_ref, out_ref)

    @pl.when(step == 0)
    def _():
        acc_ref[...] = jnp.zeros((7, 8, GRID), f32)

    mx = row_ref[0:1, :]
    mx_sq = row_ref[1:2, :]
    decay_x = row_ref[2:3, :]
    mx_back = row_ref[3:4, :]
    mod_x = row_ref[4:5, :]
    mod_x_back = row_ref[7:8, :]
    mz = col_ref[:, 0:1]
    mz_sq = col_ref[:, 1:2]
    decay_z = col_ref[:, 2:3]
    mz_back = col_ref[:, 3:4]
    mod_z = col_ref[:, 6:7]
    mod_z_back = col_ref[:, 9:10]
    for o in range(STEP):
        offset = step * STEP + o
        re = out_ref[0, o]
        im = out_ref[1, o]
        my = y_ref[0, offset]
        my_sq = y_ref[1, offset]
        decay_y = y_ref[2, offset]
        my_back = y_ref[3, offset]
        mod_y = y_ref[5, offset]
        paired = (offset >= 1) & (offset <= ROWS_B)
        mod_y_back = jnp.where(paired, y_ref[8, offset], 0.0)
        msq = mx_sq + (mz_sq + my_sq)
        anchor = msq == 0.0
        inverse = 1.0 / jnp.where(anchor, 1.0, msq)
        decay = decay_x * (decay_z * (decay_y * (1.0 / (math.pi * VOLUME))))
        base = decay * inverse * (re * re + im * im)
        base = jnp.where(anchor, 0.0, base)
        first = base * (mod_x * (mod_z * mod_y))
        second = base * (mod_x_back * (mod_z_back * mod_y_back))
        factor = (1.0 + RATE * msq) * inverse
        t1 = first * factor
        t2 = second * factor
        s1 = fold(t1)
        s2 = fold(t2)
        both = s1 + s2
        z1 = fold(t1 * mz)
        z2 = fold(t2 * mz_back)
        acc_ref[0] += fold(first + second)
        acc_ref[1] += both * mx_sq
        acc_ref[2] += both * my_sq
        acc_ref[3] += fold((t1 + t2) * mz_sq)
        acc_ref[4] += s1 * (mx * my) + s2 * (mx_back * my_back)
        acc_ref[5] += z1 * mx + z2 * mx_back
        acc_ref[6] += z1 * my + z2 * my_back

    @pl.when(step == pl.num_programs(0) - 1)
    def _():
        total = acc_ref[...]
        total = total[:, :, :128] + total[:, :, 128:256] + total[:, :, 256:384] + total[:, :, 384:]
        sum_ref[0:7, :] = total.sum(axis=1)
        sum_ref[7:8, :] = jnp.zeros((1, 128), f32)


def x_kernel_b(side_ref, g_ref, high_ref, low_ref, whole_ref, out_ref):
    del whole_ref
    x_planes(side_ref[0], g_ref, high_ref, low_ref, out_ref)


def x_specs():
    return [
        pl.BlockSpec((32, 2, STEP * 8, 128), lambda i: (0, 0, i, 0)),
        pl.BlockSpec((2, 256, GRID), lambda i: (0, 0, 0)),
        pl.BlockSpec((2, 256, GRID), lambda i: (0, 0, 0)),
    ]


OUT_SHAPE = jax.ShapeDtypeStruct((2, 16, 64, GRID), f32)


def x_stage_a(side, y_numbers, blocks, tables, row_numbers, col_numbers):
    smem = pl.BlockSpec(memory_space=pltpu.SMEM)
    return pl.pallas_call(
        x_kernel_a,
        grid=(ROWS_A // STEP,),
        in_specs=[
            smem,
            smem,
            *x_specs(),
            pl.BlockSpec((10, GRID), lambda i: (0, 0)),
            pl.BlockSpec((64, 10), lambda i: (0, 0)),
        ],
        out_specs=[
            pl.BlockSpec((2, STEP, 64, GRID), lambda i: (0, i, 0, 0)),
            pl.BlockSpec((8, 128), lambda i: (0, 0)),
        ],
        out_shape=[OUT_SHAPE, jax.ShapeDtypeStruct((8, 128), f32)],
        scratch_shapes=[pltpu.VMEM((7, 8, GRID), f32)],
        name="x_stage_a",
        cost_estimate=pl.CostEstimate(flops=4 * 10**9, bytes_accessed=6 * 10**6, transcendentals=0),
    )(side, y_numbers, blocks, *tables, row_numbers, col_numbers)


def x_stage_b(side, blocks, tables, whole):
    smem = pl.BlockSpec(memory_space=pltpu.SMEM)
    return pl.pallas_call(
        x_kernel_b,
        grid=(ROWS_B // STEP,),
        in_specs=[smem, *x_specs(), pl.BlockSpec(memory_space=pl.ANY)],
        out_specs=pl.BlockSpec((2, STEP, 64, GRID), lambda i: (0, ROWS_A // STEP + i, 0, 0)),
        out_shape=OUT_SHAPE,
        input_output_aliases={4: 0},
        name="x_stage_b",
        cost_estimate=pl.CostEstimate(flops=4 * 10**9, bytes_accessed=6 * 10**6, transcendentals=0),
    )(side, blocks, *tables, whole)


def pair_groups():
    ids = np.arange(256).reshape(32, 8)
    return [
        np.stack([ids[:, q], ids[:, 7 - q]], axis=1).reshape(-1).tolist() for q in range(4)
    ]


def exchange(blocks, rows):
    blocks = blocks.reshape(64, rows * 8, 128)
    blocks = lax.all_to_all(
        blocks, ALL, split_axis=0, concat_axis=0, tiled=True, axis_index_groups=pair_groups()
    )
    return blocks.reshape(32, 2, rows * 8, 128)


def all_sum(value):
    for axis in (("px_2",), ("px_0",), ("py_1",), ("px_1", "py_0")):
        size = lax.axis_size(axis)
        parts = [value]
        for k in range(1, size):
            parts.append(lax.ppermute(value, axis, [(s, s ^ k) for s in range(size)]))
        while len(parts) > 1:
            parts = [a + b for a, b in zip(parts[::2], parts[1::2])]
        value = parts[0]
    return value


def body(charges_old, spline_moduli):
    row_position = lax.axis_index(PX)
    col_position = lax.axis_index(PY)
    side = (col_position >= 4).astype(jnp.int32)
    planes = z_stage(charges_old[0, 0], z_table())
    planes = lax.all_to_all(planes, FIRST, split_axis=0, concat_axis=0, tiled=True)

    backward = jnp.roll(jnp.flip(spline_moduli, axis=1), 1, axis=1)
    numbers = jnp.concatenate([jnp.asarray(wave_rows()), spline_moduli, backward])
    col_numbers = lax.dynamic_slice_in_dim(numbers, col_position * 64, 64, axis=1).T
    y_numbers = lax.dynamic_slice_in_dim(numbers, row_position * 16, 16, axis=1)

    (part_a,) = y_stage(planes, range(ROWS_A), False)
    part_a = exchange(part_a, ROWS_A)
    planes, numbers, col_numbers, y_numbers = lax.optimization_barrier(
        (planes, numbers, col_numbers, y_numbers)
    )
    part_b, *tables_x = y_stage(planes, range(ROWS_A, 16), True)
    part_b = exchange(part_b, ROWS_B)

    whole, sums = x_stage_a(side.reshape(1), y_numbers, part_a, tables_x, numbers, col_numbers)
    sums = all_sum(sums).sum(axis=1)
    structure = x_stage_b(side.reshape(1), part_b, tables_x, whole)
    energy = 0.5 * sums[0]
    virial = energy * jnp.array([1.0, 1.0, 1.0, 0.0, 0.0, 0.0], dtype=f32) - sums[1:7]
    return structure, energy, virial


def solution(mesh):
    torus = Mesh(mesh.devices.reshape(4, 4, 2, 2, 4), ALL)
    return jax.shard_map(
        body,
        mesh=torus,
        in_specs=(P(PX, PY, None, None, None), P()),
        out_specs=(P(None, PX, PY, None), P(), P()),
        check_vma=False,
    )
```

profile of v0, /device:TPU:1, one launch (start us, length us, event | category | flops | bytes accessed | tf_op | source)
XLA Modules:
  0.0 180.9 jit_solution(15898662127565612004)
XLA Ops:
  0.6 6.6 %z_stage.1 = f32[16,264,128]{2,1,0:T(8,128)} custom-call(f32[32,32,512]{2,1,0:T(8,128)} %bitcast.16, bf16[512,640]{1,0:T(8,128)(2,1)} %constant.63.clone.high_ref, bf16[512,640]{1,0:T(8,128)(2,1)} %constant.64.clone.low_ref), custom_call_target="tpu_custom_call" | custom-call | flops 4000000000 | bytes 6000000 | tf_op jit(solution)/shard_map/z_stage/pallas_call | solution.py:124
  7.3 35.6 %all_to_all.15.refs_0_ = f32[16,264,128]{2,1,0:T(8,128)} all-to-all(f32[16,264,128]{2,1,0:T(8,128)} %z_stage.1), channel_id=1, replica_groups=mesh['px_0'=4,'px_1'=4,'px_2'=2,'py_0'=2,'py_1'=4] {'px_2','py_0','py_1'}, dimensions={0} | all-to-all | bytes 4325376 | tf_op jit(solution)/shard_map/all_to_all | solution.py:425
  42.9 6.7 %y_stage_10.1 = f32[5120,128]{1,0:T(8,128)} custom-call(f32[16,264,128]{2,1,0:T(8,128)} %all_to_all.15.refs_0_, f32[32,256]{1,0:T(8,128)} %constant.66.clone.refs_1_, f32[32,256]{1,0:T(8,128)} %constant.67.clone.refs_2_, f32[16,256]{1,0:T(8,128)} %constant.68.clone.refs_3_, f32[16,256]{1,0:T(8,128)} %constant.69.clone.refs_4_), custom_call_target="tpu_custom_call" | custom-call | flops 4000000000 | bytes 6000000 | tf_op jit(solution)/shard_map/y_stage_10/pallas_call | solution.py:232
  49.6 11.1 %all-to-all-start.2 = ((f32[64,80,128]{2,1,0:T(8,128)}), f32[64,80,128]{2,1,0:T(8,128)S(1)}, u32[]{:S(2)}, u32[]{:S(2)}) async-start(f32[64,80,128]{2,1,0:T(8,128)} %bitcast.11), calls=%async_computation.2 | async-start | bytes 5242880 | tf_op jit(solution)/shard_map/all_to_all | solution.py:402
  60.8 0.4 reverse.2
  61.4 0.7 copy.28
  62.1 0.7 constant_dynamic-slice_fusion.y_ref
  62.8 5.4 %y_stage_6.1 = (f32[3072,128]{1,0:T(8,128)}, bf16[2,256,512]{2,1,0:T(8,128)(2,1)}, bf16[2,256,512]{2,1,0:T(8,128)(2,1)}) custom-call(f32[16,264,128]{2,1,0:T(8,128)} %all_to_all.15.refs_0_, f32[32,256]{1,0:T(8,128)} %constant.66.clone.refs_1_, f32[32,256]{1,0:T(8,128)} %constant.67.clone.refs_2_, f32[16,256]{1,0:T(8,128)} %constant.68.clone.refs_3_, ...), custom_call_target="tpu_custom_call" | custom-call | flops 4000000000 | bytes 6000000 | tf_op jit(solution)/shard_map/y_stage_6/pallas_call | solution.py:232
  68.2 56.0 %all-to-all-done.2 = f32[64,80,128]{2,1,0:T(8,128)S(1)} async-done(((f32[64,80,128]{2,1,0:T(8,128)}), f32[64,80,128]{2,1,0:T(8,128)S(1)}, u32[]{:S(2)}, u32[]{:S(2)}) %all-to-all-start.2) | async-done | bytes 2621472 | tf_op jit(solution)/shard_map/all_to_all | solution.py:402
  124.2 7.1 %all-to-all-start.1 = ((f32[64,48,128]{2,1,0:T(8,128)}), f32[64,48,128]{2,1,0:T(8,128)}, u32[]{:S(2)}, u32[]{:S(2)}) async-start(f32[64,48,128]{2,1,0:T(8,128)} %bitcast.12), calls=%async_computation.1 | async-start | bytes 3145728 | tf_op jit(solution)/shard_map/all_to_all | solution.py:402
  131.4 8.0 %x_stage_a.1 = (f32[2,16,64,512]{3,2,1,0:T(8,128)}, f32[8,128]{1,0:T(8,128)}) custom-call(s32[1]{0:T(128)} %bitcast.side_ref, f32[10,16]{1,0:T(8,128)} %constant_dynamic-slice_fusion.y_ref, f32[32,2,80,128]{3,2,1,0:T(8,128)} %bitcast.10, bf16[2,256,512]{2,1,0:T(8,128)(2,1)} %get-tuple-element.14.high_ref, bf16[2,256,512]{2,1,0:T(8,128)(2,1)} %get-tuple-element.15.low_ref, ...), custom_call_target="tpu_custom_call" | custom-call | flops 4000000000 | bytes 6000000 | tf_op jit(solution)/shard_map/x_stage_a/pallas_call | solution.py:358
  139.3 0.5 collective-permute-start
  139.9 1.0 collective-permute-done
  140.9 0.7 add.62
  141.6 1.2 collective-permute-start.1
  142.8 2.6 %collective-permute-start.2 = (f32[8,128]{1,0:T(8,128)S(1)}, f32[8,128]{1,0:T(8,128)S(1)}, u32[]{:S(2)}, u32[]{:S(2)}) collective-permute-start(f32[8,128]{1,0:T(8,128)S(1)} %add.62), channel_id=1, source_target_pairs={{0,128},{64,192},{128,0},{192,64},{1,129},{65,193},{129,1},{193,65... | collective-permute-start | bytes 12296 | tf_op jit(solution)/shard_map/ppermute | solution.py:413
  145.4 1.7 collective-permute-done.2
  147.2 2.5 %collective-permute-done.3 = f32[8,128]{1,0:T(8,128)S(1)} collective-permute-done((f32[8,128]{1,0:T(8,128)S(1)}, f32[8,128]{1,0:T(8,128)S(1)}, u32[]{:S(2)}, u32[]{:S(2)}) %collective-permute-start.3) | collective-permute-done | bytes 4128 | tf_op jit(solution)/shard_map/ppermute | solution.py:413
  149.7 2.7 %collective-permute-start.5 = (f32[8,128]{1,0:T(8,128)S(1)}, f32[8,128]{1,0:T(8,128)S(1)}, u32[]{:S(2)}, u32[]{:S(2)}) collective-permute-start(f32[8,128]{1,0:T(8,128)S(1)} %add_add_fusion.1), channel_id=1, source_target_pairs={{0,2},{1,3},{2,0},{3,1},{4,6},{5,7},{6,4},{7,5},{8,10},{9,11},{10,... | collective-permute-start | bytes 12296 | tf_op jit(solution)/shard_map/ppermute | solution.py:413
  152.4 1.1 collective-permute-start.6
  153.5 0.8 collective-permute-done.5
  154.3 2.2 %collective-permute-done.6 = f32[8,128]{1,0:T(8,128)S(1)} collective-permute-done((f32[8,128]{1,0:T(8,128)S(1)}, f32[8,128]{1,0:T(8,128)S(1)}, u32[]{:S(2)}, u32[]{:S(2)}) %collective-permute-start.6) | collective-permute-done | bytes 4128 | tf_op jit(solution)/shard_map/ppermute | solution.py:413
  156.5 5.1 %collective-permute-start.10 = (f32[8,128]{1,0:T(8,128)S(1)}, f32[8,128]{1,0:T(8,128)S(1)}, u32[]{:S(2)}, u32[]{:S(2)}) collective-permute-start(f32[8,128]{1,0:T(8,128)S(1)} %add_add_fusion), channel_id=1, source_target_pairs={{0,32},{4,36},{16,48},{20,52},{32,0},{36,4},{48,16},{52,20},{1,33}... | collective-permute-start | bytes 12296 | tf_op jit(solution)/shard_map/ppermute | solution.py:413
  161.6 1.1 collective-permute-start.11
  162.7 2.4 %collective-permute-start.12 = (f32[8,128]{1,0:T(8,128)S(1)}, f32[8,128]{1,0:T(8,128)S(1)}, u32[]{:S(2)}, u32[]{:S(2)}) collective-permute-start(f32[8,128]{1,0:T(8,128)S(1)} %add_add_fusion), channel_id=1, source_target_pairs={{0,48},{4,52},{16,32},{20,36},{32,16},{36,20},{48,0},{52,4},{1,49}... | collective-permute-start | bytes 12296 | tf_op jit(solution)/shard_map/ppermute | solution.py:413
  165.0 2.4 %collective-permute-start.7 = (f32[8,128]{1,0:T(8,128)S(1)}, f32[8,128]{1,0:T(8,128)S(1)}, u32[]{:S(2)}, u32[]{:S(2)}) collective-permute-start(f32[8,128]{1,0:T(8,128)S(1)} %add_add_fusion), channel_id=1, source_target_pairs={{0,4},{4,0},{16,20},{20,16},{32,36},{36,32},{48,52},{52,48},{1,5},... | collective-permute-start | bytes 12296 | tf_op jit(solution)/shard_map/ppermute | solution.py:413
  167.4 1.3 collective-permute-done.10
  168.7 0.8 collective-permute-start.8
  169.5 1.6 collective-permute-done.11
  171.1 3.0 %collective-permute-start.9 = (f32[8,128]{1,0:T(8,128)S(1)}, f32[8,128]{1,0:T(8,128)S(1)}, u32[]{:S(2)}, u32[]{:S(2)}) collective-permute-start(f32[8,128]{1,0:T(8,128)S(1)} %add_add_fusion), channel_id=1, source_target_pairs={{0,20},{4,16},{16,4},{20,0},{32,52},{36,48},{48,36},{52,32},{1,21}... | collective-permute-start | bytes 12296 | tf_op jit(solution)/shard_map/ppermute | solution.py:413
  174.1 4.8 %x_stage_b.1 = f32[2,16,64,512]{3,2,1,0:T(8,128)} custom-call(s32[1]{0:T(128)} %bitcast.side_ref, f32[32,2,48,128]{3,2,1,0:T(8,128)} %bitcast.4.g_ref, bf16[2,256,512]{2,1,0:T(8,128)(2,1)} %get-tuple-element.14.high_ref, bf16[2,256,512]{2,1,0:T(8,128)(2,1)} %get-tuple-element.15.low_ref, ...), custom_call_target="tpu_custom_call", output_to_operand_aliasing={{}: (4, {})} | custom-call | flops 4000000000 | bytes 6000000 | tf_op jit(solution)/shard_map/x_stage_b/pallas_call | solution.py:381
  179.2 0.6 slice_subtract_fusion
  (30 shorter events, 0.5 us)
Async XLA Ops:
  49.6 11.1 %copy-start.2 = (f32[3,512]{1,0:T(4,128)S(1)}, f32[3,512]{1,0:T(4,128)}, u32[]{:S(2)}) copy-start(f32[3,512]{1,0:T(4,128)} %param.19) | copy-start | bytes 18436
  49.6 11.6 %slice-start = ((f32[3,512]{1,0:T(4,128)}), f32[3,1]{1,0:T(4,128)S(1)}, s32[]{:S(2)}) async-start(f32[3,512]{1,0:T(4,128)} %param.19), calls=%async_computation.3 | async-start | bytes 4096 | tf_op jit(solution)/shard_map/jit(_roll_static)/slice | solution.py:427
  49.6 11.6 %copy-start.3 = (f32[4,512]{1,0:T(4,128)S(1)}, f32[4,512]{1,0:T(4,128)}, u32[]{:S(2)}) copy-start(f32[4,512]{1,0:T(4,128)} %constant.65.clone) | copy-start | bytes 24580
  49.6 74.6 %all-to-all-start.2 = ((f32[64,80,128]{2,1,0:T(8,128)}), f32[64,80,128]{2,1,0:T(8,128)S(1)}, u32[]{:S(2)}, u32[]{:S(2)}) async-start(f32[64,80,128]{2,1,0:T(8,128)} %bitcast.11), calls=%async_computation.2 | async-start | bytes 5242880 | tf_op jit(solution)/shard_map/all_to_all | solution.py:402
  61.3 6.9 %copy-start.1 = (f32[10,512]{1,0:T(8,128)}, f32[10,512]{1,0:T(8,128)S(1)}, u32[]{:S(2)}) copy-start(f32[10,512]{1,0:T(8,128)S(1)} %maximum_maximum_fusion.row_ref) | copy-start | bytes 61444
  124.2 7.2 %copy-start = (f32[64,80,128]{2,1,0:T(8,128)}, f32[64,80,128]{2,1,0:T(8,128)S(1)}, u32[]{:S(2)}) copy-start(f32[64,80,128]{2,1,0:T(8,128)S(1)} %all-to-all-done.2) | copy-start | bytes 7864324
  124.2 49.9 %all-to-all-start.1 = ((f32[64,48,128]{2,1,0:T(8,128)}), f32[64,48,128]{2,1,0:T(8,128)}, u32[]{:S(2)}, u32[]{:S(2)}) async-start(f32[64,48,128]{2,1,0:T(8,128)} %bitcast.12), calls=%async_computation.1 | async-start | bytes 3145728 | tf_op jit(solution)/shard_map/all_to_all | solution.py:402
  139.3 1.6 collective-permute-start
  141.6 3.9 %collective-permute-start.1 = (f32[8,128]{1,0:T(8,128)S(1)}, f32[8,128]{1,0:T(8,128)S(1)}, u32[]{:S(2)}, u32[]{:S(2)}) collective-permute-start(f32[8,128]{1,0:T(8,128)S(1)} %add.62), channel_id=1, source_target_pairs={{0,64},{64,0},{128,192},{192,128},{1,65},{65,1},{129,193},{193,129... | collective-permute-start | bytes 12296 | tf_op jit(solution)/shard_map/ppermute | solution.py:413
  142.8 4.4 %collective-permute-start.2 = (f32[8,128]{1,0:T(8,128)S(1)}, f32[8,128]{1,0:T(8,128)S(1)}, u32[]{:S(2)}, u32[]{:S(2)}) collective-permute-start(f32[8,128]{1,0:T(8,128)S(1)} %add.62), channel_id=1, source_target_pairs={{0,128},{64,192},{128,0},{192,64},{1,129},{65,193},{129,1},{193,65... | collective-permute-start | bytes 12296 | tf_op jit(solution)/shard_map/ppermute | solution.py:413
  145.4 4.2 %collective-permute-start.3 = (f32[8,128]{1,0:T(8,128)S(1)}, f32[8,128]{1,0:T(8,128)S(1)}, u32[]{:S(2)}, u32[]{:S(2)}) collective-permute-start(f32[8,128]{1,0:T(8,128)S(1)} %add.62), channel_id=1, source_target_pairs={{0,192},{64,128},{128,64},{192,0},{1,193},{65,129},{129,65},{193,1... | collective-permute-start | bytes 12296 | tf_op jit(solution)/shard_map/ppermute | solution.py:413
  149.7 3.9 %collective-permute-start.4 = (f32[8,128]{1,0:T(8,128)S(1)}, f32[8,128]{1,0:T(8,128)S(1)}, u32[]{:S(2)}, u32[]{:S(2)}) collective-permute-start(f32[8,128]{1,0:T(8,128)S(1)} %add_add_fusion.1), channel_id=1, source_target_pairs={{0,1},{1,0},{2,3},{3,2},{4,5},{5,4},{6,7},{7,6},{8,9},{9,8},{10,11... | collective-permute-start | bytes 12296 | tf_op jit(solution)/shard_map/ppermute | solution.py:413
  149.7 4.6 %collective-permute-start.5 = (f32[8,128]{1,0:T(8,128)S(1)}, f32[8,128]{1,0:T(8,128)S(1)}, u32[]{:S(2)}, u32[]{:S(2)}) collective-permute-start(f32[8,128]{1,0:T(8,128)S(1)} %add_add_fusion.1), channel_id=1, source_target_pairs={{0,2},{1,3},{2,0},{3,1},{4,6},{5,7},{6,4},{7,5},{8,10},{9,11},{10,... | collective-permute-start | bytes 12296 | tf_op jit(solution)/shard_map/ppermute | solution.py:413
  152.4 4.1 %collective-permute-start.6 = (f32[8,128]{1,0:T(8,128)S(1)}, f32[8,128]{1,0:T(8,128)S(1)}, u32[]{:S(2)}, u32[]{:S(2)}) collective-permute-start(f32[8,128]{1,0:T(8,128)S(1)} %add_add_fusion.1), channel_id=1, source_target_pairs={{0,3},{1,2},{2,1},{3,0},{4,7},{5,6},{6,5},{7,4},{8,11},{9,10},{10,... | collective-permute-start | bytes 12296 | tf_op jit(solution)/shard_map/ppermute | solution.py:413
  156.5 12.3 %collective-permute-start.10 = (f32[8,128]{1,0:T(8,128)S(1)}, f32[8,128]{1,0:T(8,128)S(1)}, u32[]{:S(2)}, u32[]{:S(2)}) collective-permute-start(f32[8,128]{1,0:T(8,128)S(1)} %add_add_fusion), channel_id=1, source_target_pairs={{0,32},{4,36},{16,48},{20,52},{32,0},{36,4},{48,16},{52,20},{1,33}... | collective-permute-start | bytes 12296 | tf_op jit(solution)/shard_map/ppermute | solution.py:413
  161.6 9.5 %collective-permute-start.11 = (f32[8,128]{1,0:T(8,128)S(1)}, f32[8,128]{1,0:T(8,128)S(1)}, u32[]{:S(2)}, u32[]{:S(2)}) collective-permute-start(f32[8,128]{1,0:T(8,128)S(1)} %add_add_fusion), channel_id=1, source_target_pairs={{0,36},{4,32},{16,52},{20,48},{32,4},{36,0},{48,20},{52,16},{1,37}... | collective-permute-start | bytes 12296 | tf_op jit(solution)/shard_map/ppermute | solution.py:413
  162.7 16.3 %collective-permute-start.12 = (f32[8,128]{1,0:T(8,128)S(1)}, f32[8,128]{1,0:T(8,128)S(1)}, u32[]{:S(2)}, u32[]{:S(2)}) collective-permute-start(f32[8,128]{1,0:T(8,128)S(1)} %add_add_fusion), channel_id=1, source_target_pairs={{0,48},{4,52},{16,32},{20,36},{32,16},{36,20},{48,0},{52,4},{1,49}... | collective-permute-start | bytes 12296 | tf_op jit(solution)/shard_map/ppermute | solution.py:413
  165.0 13.9 %collective-permute-start.13 = (f32[8,128]{1,0:T(8,128)S(1)}, f32[8,128]{1,0:T(8,128)S(1)}, u32[]{:S(2)}, u32[]{:S(2)}) collective-permute-start(f32[8,128]{1,0:T(8,128)S(1)} %add_add_fusion), channel_id=1, source_target_pairs={{0,52},{4,48},{16,36},{20,32},{32,20},{36,16},{48,4},{52,0},{1,53}... | collective-permute-start | bytes 12296 | tf_op jit(solution)/shard_map/ppermute | solution.py:413
  165.0 13.9 %collective-permute-start.7 = (f32[8,128]{1,0:T(8,128)S(1)}, f32[8,128]{1,0:T(8,128)S(1)}, u32[]{:S(2)}, u32[]{:S(2)}) collective-permute-start(f32[8,128]{1,0:T(8,128)S(1)} %add_add_fusion), channel_id=1, source_target_pairs={{0,4},{4,0},{16,20},{20,16},{32,36},{36,32},{48,52},{52,48},{1,5},... | collective-permute-start | bytes 12296 | tf_op jit(solution)/shard_map/ppermute | solution.py:413
  168.7 10.2 %collective-permute-start.8 = (f32[8,128]{1,0:T(8,128)S(1)}, f32[8,128]{1,0:T(8,128)S(1)}, u32[]{:S(2)}, u32[]{:S(2)}) collective-permute-start(f32[8,128]{1,0:T(8,128)S(1)} %add_add_fusion), channel_id=1, source_target_pairs={{0,16},{4,20},{16,0},{20,4},{32,48},{36,52},{48,32},{52,36},{1,17}... | collective-permute-start | bytes 12296 | tf_op jit(solution)/shard_map/ppermute | solution.py:413
  171.1 7.9 %collective-permute-start.9 = (f32[8,128]{1,0:T(8,128)S(1)}, f32[8,128]{1,0:T(8,128)S(1)}, u32[]{:S(2)}, u32[]{:S(2)}) collective-permute-start(f32[8,128]{1,0:T(8,128)S(1)} %add_add_fusion), channel_id=1, source_target_pairs={{0,20},{4,16},{16,4},{20,0},{32,52},{36,48},{48,36},{52,32},{1,21}... | collective-permute-start | bytes 12296 | tf_op jit(solution)/shard_map/ppermute | solution.py:413
  174.1 5.1 %copy-start.4 = (f32[6]{0:T(128)S(1)}, f32[6]{0:T(128)}, u32[]{:S(2)}) copy-start(f32[6]{0:T(128)} %constant.74.clone) | copy-start | bytes 76
where the time goes:
time: 182 us; the launch traced here: 181 us
  waiting for transfers between devices  67.1 us (37%)
  starting transfers between devices  41.1 us (23%)
  blocking collectives  35.6 us (20%)
  Pallas kernels  31.6 us (17%)
  local copies, waits for them, and re-layouts  1.98 us (1%)
  between operations  1.91 us (1%)
    all_to_all x2, waiting for transfers between devices, exchange(): lax.all_to_all(blocks, ALL, split_axis=0, concat_axis=0, tiled=True, axis...  56 us
    all_to_all x1, blocking collectives, body(): lax.all_to_all(planes, FIRST, split_axis=0, concat_axis=0, tiled=True)  35.6 us
    ppermute x14, starting transfers between devices, all_sum(): parts.append(lax.ppermute(value, axis, [(s, s ^ k) for s in range(size)]))  22.9 us
    all_to_all x2, starting transfers between devices, exchange(): lax.all_to_all(blocks, ALL, split_axis=0, concat_axis=0, tiled=True, axis...  18.2 us
    pallas_call x2, Pallas kernels, y_stage(): pl.pallas_call(kernel, in_specs=[whole] * len(inputs), out_specs=[whole]...  12.2 us
    ppermute x14, waiting for transfers between devices, all_sum(): parts.append(lax.ppermute(value, axis, [(s, s ^ k) for s in range(size)]))  11.1 us
    pallas_call x1, Pallas kernels, x_stage_a(): pl.pallas_call(x_kernel_a, grid=(ROWS_A // STEP,), in_specs=[smem, smem,...  7.98 us
    pallas_call x1, Pallas kernels, z_stage(): pl.pallas_call(z_kernel, grid=(4,), in_specs=[pl.BlockSpec((8, 32, GRID),...  6.64 us
  transfers between devices with their start and end apart: 16, of which 8 were waited for; matrix products, arithmetic and copies ran while one was open for 2% of the time, Pallas kernels for 10%

commit v1 on v0

--- a/solution.py
+++ b/solution.py
@@ -130,29 +130,35 @@
             pl.BlockSpec((GRID, 640), lambda i: (0, 0)),
         ],
         out_specs=pl.BlockSpec((16, EXT, 128), lambda i: (0, 0, 0)),
-        out_shape=jax.ShapeDtypeStruct((16, EXT, 128), f32),
+        out_shape=pltpu.MemorySpace.VMEM((16, EXT, 128), f32),
         scratch_shapes=[pltpu.VMEM((16, 8, 128), f32)],
         name="z_stage",
         cost_estimate=pl.CostEstimate(flops=4 * 10**9, bytes_accessed=6 * 10**6, transcendentals=0),
     )(block, *tables)
 
 
-def y_kernel(offsets, g_ref, pc_ref, ps_ref, oc_ref, os_ref, out_ref):
+def y_rows(offsets, parts, g_ref, factor_refs, stage_ref, ready, deliver):
+    pc_ref, ps_ref, oc_ref, os_ref = factor_refs
     rows = len(offsets)
-    lane = lane_index((32, 128))
+    size = 32 // parts
+    pitch = rows * 64 + 8
+    lane = lane_index((size, 128))
     real = lane // 32 % 2 == 0
     back = lane // 32 * 32 + (32 - lane % 32) % 32
     slot = lane % 32 == 0
     groups = [[o for o in offsets if o % 2 == parity] for parity in range(2)]
-    pc = pc_ref[...]
-    ps = ps_ref[...]
-    tables = []
-    for group in groups:
-        cosines = [pc * oc_ref[o : o + 1, :] - ps * os_ref[o : o + 1, :] for o in group]
-        sines = [ps * oc_ref[o : o + 1, :] + pc * os_ref[o : o + 1, :] for o in group]
-        tables.append(halves(jnp.concatenate(cosines + sines, axis=0)))
-
-    def products(low, high):
+
+    def tables_of(part):
+        pc = pc_ref[part * size : part * size + size, :]
+        ps = ps_ref[part * size : part * size + size, :]
+        tables = []
+        for group in groups:
+            cosines = [pc * oc_ref[o : o + 1, :] - ps * os_ref[o : o + 1, :] for o in group]
+            sines = [ps * oc_ref[o : o + 1, :] + pc * os_ref[o : o + 1, :] for o in group]
+            tables.append(halves(jnp.concatenate(cosines + sines, axis=0)))
+        return tables
+
+    def products(tables, low, high):
         results = []
         for (t_high, t_low), g in zip(tables, (low + high, low - high)):
             g_high, g_low = halves(g)
@@ -161,45 +167,148 @@
 
     def pieces(results, columns):
         for parity, group in enumerate(groups):
-            count = len(group) * 32
+            count = len(group) * size
             for k, o in enumerate(group):
-                p = results[parity][k * 32 : k * 32 + 32, columns]
-                q = results[parity][count + k * 32 : count + k * 32 + 32, columns]
+                p = results[parity][k * size : k * size + size, columns]
+                q = results[parity][count + k * size : count + k * size + size, columns]
                 turned = jnp.where(real, pltpu.roll(q, 96, 1), -pltpu.roll(q, 32, 1))
                 other = p - turned
                 yield offsets.index(o), p + turned, jnp.where(real, other, -other)
 
     def unpacked(start):
-        parts = []
+        blocks = []
         for s in range(start, start + 8):
             packed = g_ref[s, 256:EXT, :]
             for quarter in range(4):
-                parts.append(pltpu.roll(packed, 128 - 8 * quarter, 1) if quarter else packed)
-        return jnp.concatenate(parts, axis=0)
-
-    extra = {k: m for k, _, m in pieces(products(unpacked(0), unpacked(8)), slice(0, 128))}
-
-    for pair in range(4):
-        sides = []
-        for start in (0, 8):
-            columns = [
-                g_ref[start : start + 8, x2 * 32 : x2 * 32 + 32, :].reshape(256, 128)
-                for x2 in (2 * pair, 2 * pair + 1)
-            ]
-            sides.append(jnp.concatenate(columns, axis=1))
-        results = products(*sides)
-        for x2 in (2 * pair, 2 * pair + 1):
-            first = x2 % 2 * 128
-            for k, direct, mirror in pieces(results, slice(first, first + 128)):
-                moved = pltpu.roll(extra[k], 128 - x2, 1) if x2 else extra[k]
-                mirror = jnp.where(slot, moved, mirror)
-                mirror = jnp.take_along_axis(mirror, back, axis=1)
-                stride = 2 * rows * 8
-                out_ref[pl.ds(k * 8 + x2, 32, stride=stride), :] = direct
-                out_ref[pl.ds((rows + k) * 8 + x2, 32, stride=stride), :] = mirror
-
-
-def x_table_rows(ac_ref, as_ref, bc_ref, bs_ref, high_ref, low_ref):
+                blocks.append(pltpu.roll(packed, 128 - 8 * quarter, 1) if quarter else packed)
+        return jnp.concatenate(blocks, axis=0)
+
+    for part in range(parts):
+        tables = tables_of(part)
+        ready(4, part)
+        results = products(tables, unpacked(0), unpacked(8))
+        extra = {k: m for k, _, m in pieces(results, slice(0, 128))}
+        for pair in range(4):
+            ready(pair, part)
+            sides = []
+            for start in (0, 8):
+                columns = [
+                    g_ref[start : start + 8, x2 * 32 : x2 * 32 + 32, :].reshape(256, 128)
+                    for x2 in (2 * pair, 2 * pair + 1)
+                ]
+                sides.append(jnp.concatenate(columns, axis=1))
+            results = products(tables, *sides)
+            for x2 in (2 * pair, 2 * pair + 1):
+                first = x2 % 2 * 128
+                for k, direct, mirror in pieces(results, slice(first, first + 128)):
+                    moved = pltpu.roll(extra[k], 128 - x2, 1) if x2 else extra[k]
+                    mirror = jnp.where(slot, moved, mirror)
+                    mirror = jnp.take_along_axis(mirror, back, axis=1)
+                    at = x2 * pitch + k * 32 + part * size
+                    stage_ref[at : at + size, :] = direct
+                    stage_ref[at + rows * 32 : at + rows * 32 + size, :] = mirror
+        deliver(part)
+
+
+def y_kernel_a(offsets, g_ref, pc_ref, ps_ref, oc_ref, os_ref, target_ref, copy_ref, out_ref, stage_ref, copy_sem, out_sems):
+    rows = len(offsets)
+    pitch = rows * 64 + 8
+    copy = pltpu.make_async_copy(g_ref, copy_ref, copy_sem)
+    copy.start()
+
+    def flush(part):
+        window = pl.ds(part * 32, 32)
+        return pltpu.make_async_copy(out_ref.at[window], target_ref.at[window], out_sems.at[part])
+
+    def gather(p, carry):
+        for pair in range(2):
+            for k in range(rows):
+                first = (pair * rows + k) * 32 + p
+                block = stage_ref[pl.ds(first, 8, stride=pitch), :]
+                out_ref[2 * p + pair, k * 8 : k * 8 + 8, :] = block
+        return carry
+
+    def deliver(part):
+        lax.fori_loop(part * 16, part * 16 + 16, gather, 0)
+        flush(part).start()
+
+    factors = (pc_ref, ps_ref, oc_ref, os_ref)
+    y_rows(offsets, 2, g_ref, factors, stage_ref, lambda *_: None, deliver)
+    copy.wait()
+    flush(0).wait()
+    flush(1).wait()
+
+
+def y_kernel_b(offsets, core_ref, g_ref, pc_ref, ps_ref, oc_ref, os_ref, keep_ref, send_ref, stage_ref):
+    rows = len(offsets)
+    pitch = rows * 64 + 8
+    core = core_ref[0]
+
+    def gather(p, carry):
+        for out_ref, side in ((keep_ref, core), (send_ref, 1 - core)):
+            for pair in range(2):
+                for k in range(rows):
+                    first = (pair * rows + k) * 32 + 2 * p + side
+                    block = stage_ref[pl.ds(first, 8, stride=pitch), :]
+                    out_ref[2 * p + pair, k * 8 : k * 8 + 8, :] = block
+        return carry
+
+    def deliver(part):
+        lax.fori_loop(0, 16, gather, 0)
+
+    factors = (pc_ref, ps_ref, oc_ref, os_ref)
+    y_rows(offsets, 1, g_ref, factors, stage_ref, lambda *_: None, deliver)
+
+
+WHOLE = pl.BlockSpec(memory_space=pltpu.VMEM)
+SMALL = pltpu.CompilerParams(vmem_limit_bytes=24 * 2**20)
+
+
+def y_stage_a(blocks):
+    rows = ROWS_A
+
+    def kernel(*refs):
+        y_kernel_a(list(range(ROWS_A)), *refs)
+
+    hbm = pl.BlockSpec(memory_space=pltpu.HBM)
+    return pl.pallas_call(
+        kernel,
+        in_specs=[WHOLE] * 5,
+        out_specs=[hbm, hbm],
+        out_shape=[
+            pltpu.MemorySpace.HBM((64, rows * 8, 128), f32),
+            pltpu.MemorySpace.HBM((16, EXT, 128), f32),
+        ],
+        scratch_shapes=[
+            pltpu.VMEM((64, rows * 8, 128), f32),
+            pltpu.VMEM((8 * (rows * 64 + 8), 128), f32),
+            pltpu.SemaphoreType.DMA,
+            pltpu.SemaphoreType.DMA((2,)),
+        ],
+        compiler_params=SMALL,
+        name="y_stage_a",
+        cost_estimate=pl.CostEstimate(flops=4 * 10**9, bytes_accessed=6 * 10**6, transcendentals=0),
+    )(blocks, *y_factors())
+
+
+def y_stage_b(core, blocks):
+    rows = ROWS_B
+
+    def kernel(*refs):
+        y_kernel_b(list(range(ROWS_A, 16)), *refs)
+
+    return pl.pallas_call(
+        kernel,
+        in_specs=[pl.BlockSpec(memory_space=pltpu.SMEM)] + [WHOLE] * 5,
+        out_specs=[WHOLE, WHOLE],
+        out_shape=[jax.ShapeDtypeStruct((32, rows * 8, 128), f32)] * 2,
+        scratch_shapes=[pltpu.VMEM((8 * (rows * 64 + 8), 128), f32)],
+        name="y_stage_b",
+        cost_estimate=pl.CostEstimate(flops=4 * 10**9, bytes_accessed=6 * 10**6, transcendentals=0),
+    )(core, blocks, *y_factors())
+
+
+def x_tables(ac_ref, as_ref, bc_ref, bs_ref, high_ref, low_ref):
     for parity in range(2):
         bc = bc_ref[parity * 16 : parity * 16 + 16, :]
         bs = bs_ref[parity * 16 : parity * 16 + 16, :]
@@ -212,38 +321,41 @@
             low_ref[parity, a * 16 : a * 16 + 16, :] = low
 
 
-def y_stage(blocks, offsets, with_tables):
+def y_stage(blocks, offsets):
     offsets = list(offsets)
     rows = len(offsets)
 
     def kernel(*refs):
-        if with_tables:
-            y_kernel(offsets, *refs[:5], refs[9])
-            x_table_rows(*refs[5:9], *refs[10:])
-        else:
-            y_kernel(offsets, *refs)
-
-    inputs = [blocks, *y_factors()]
-    out_shape = [jax.ShapeDtypeStruct((64 * rows * 8, 128), f32)]
-    if with_tables:
-        inputs += x_factors()
-        out_shape += [jax.ShapeDtypeStruct((2, 256, GRID), bf16)] * 2
+        y_kernel(offsets, *refs)
+
     whole = pl.BlockSpec(memory_space=pltpu.VMEM)
+    hbm = pl.BlockSpec(memory_space=pltpu.HBM)
     return pl.pallas_call(
         kernel,
-        in_specs=[whole] * len(inputs),
-        out_specs=[whole] * len(out_shape),
-        out_shape=out_shape,
+        in_specs=[hbm] + [whole] * 4,
+        out_specs=hbm,
+        out_shape=jax.ShapeDtypeStruct((64, rows * 8, 128), f32),
+        scratch_shapes=[
+            pltpu.VMEM((16, EXT, 128), f32),
+            pltpu.VMEM((64, rows * 8, 128), f32),
+            pltpu.VMEM((8 * (rows * 64 + 8), 128), f32),
+            pltpu.SemaphoreType.DMA((5,)),
+            pltpu.SemaphoreType.DMA((4,)),
+        ],
         name=f"y_stage_{rows}",
         cost_estimate=pl.CostEstimate(flops=4 * 10**9, bytes_accessed=6 * 10**6, transcendentals=0),
-    )(*inputs)
+    )(blocks, *y_factors())
 
 
 def x_planes(high, g_ref, high_ref, low_ref, out_ref):
     turned = {}
     for o in range(STEP):
         for s in range(2):
-            block = g_ref[:, s, o * 8 : o * 8 + 8, :].reshape(256, 128)
+            if len(g_ref.shape) == 5:
+                block = g_ref[:, s, :, o * 8 : o * 8 + 8, :]
+            else:
+                block = g_ref[:, s, o * 8 : o * 8 + 8, :]
+            block = block.reshape(256, 128)
             turned[o, s] = jnp.transpose(block)
     half = STEP * 64
     real = []
@@ -274,8 +386,13 @@
     return value.reshape(8, 8, GRID).sum(axis=0)
 
 
-def x_kernel_a(side_ref, y_ref, g_ref, high_ref, low_ref, row_ref, col_ref, out_ref, sum_ref, acc_ref):
+def x_kernel_a(side_ref, y_ref, g_ref, ac_ref, as_ref, bc_ref, bs_ref, row_ref, col_ref, out_ref, sum_ref, acc_ref, high_ref, low_ref):
     step = pl.program_id(0)
+
+    @pl.when(step == 0)
+    def _():
+        x_tables(ac_ref, as_ref, bc_ref, bs_ref, high_ref, low_ref)
+
     x_planes(side_ref[0], g_ref, high_ref, low_ref, out_ref)
 
     @pl.when(step == 0)
@@ -337,23 +454,22 @@
         sum_ref[7:8, :] = jnp.zeros((1, 128), f32)
 
 
-def x_kernel_b(side_ref, g_ref, high_ref, low_ref, whole_ref, out_ref):
+def x_kernel_b(side_ref, g_ref, ac_ref, as_ref, bc_ref, bs_ref, whole_ref, out_ref, high_ref, low_ref):
     del whole_ref
+
+    @pl.when(pl.program_id(0) == 0)
+    def _():
+        x_tables(ac_ref, as_ref, bc_ref, bs_ref, high_ref, low_ref)
+
     x_planes(side_ref[0], g_ref, high_ref, low_ref, out_ref)
 
 
-def x_specs():
-    return [
-        pl.BlockSpec((32, 2, STEP * 8, 128), lambda i: (0, 0, i, 0)),
-        pl.BlockSpec((2, 256, GRID), lambda i: (0, 0, 0)),
-        pl.BlockSpec((2, 256, GRID), lambda i: (0, 0, 0)),
-    ]
-
-
+FACTORS = [pl.BlockSpec((rows, 256), lambda i: (0, 0)) for rows in (16, 16, 32, 32)]
+TABLES = [pltpu.VMEM((2, 256, GRID), bf16)] * 2
 OUT_SHAPE = jax.ShapeDtypeStruct((2, 16, 64, GRID), f32)
 
 
-def x_stage_a(side, y_numbers, blocks, tables, row_numbers, col_numbers):
+def x_stage_a(side, y_numbers, blocks, row_numbers, col_numbers):
     smem = pl.BlockSpec(memory_space=pltpu.SMEM)
     return pl.pallas_call(
         x_kernel_a,
@@ -361,7 +477,8 @@
         in_specs=[
             smem,
             smem,
-            *x_specs(),
+            pl.BlockSpec((32, 2, STEP * 8, 128), lambda i: (0, 0, i, 0)),
+            *FACTORS,
             pl.BlockSpec((10, GRID), lambda i: (0, 0)),
             pl.BlockSpec((64, 10), lambda i: (0, 0)),
         ],
@@ -370,43 +487,54 @@
             pl.BlockSpec((8, 128), lambda i: (0, 0)),
         ],
         out_shape=[OUT_SHAPE, jax.ShapeDtypeStruct((8, 128), f32)],
-        scratch_shapes=[pltpu.VMEM((7, 8, GRID), f32)],
+        scratch_shapes=[pltpu.VMEM((7, 8, GRID), f32), *TABLES],
+        compiler_params=pltpu.CompilerParams(vmem_limit_bytes=24 * 2**20),
         name="x_stage_a",
         cost_estimate=pl.CostEstimate(flops=4 * 10**9, bytes_accessed=6 * 10**6, transcendentals=0),
-    )(side, y_numbers, blocks, *tables, row_numbers, col_numbers)
-
-
-def x_stage_b(side, blocks, tables, whole):
+    )(side, y_numbers, blocks, *x_factors(), row_numbers, col_numbers)
+
+
+def x_stage_b(side, blocks, whole):
     smem = pl.BlockSpec(memory_space=pltpu.SMEM)
     return pl.pallas_call(
         x_kernel_b,
         grid=(ROWS_B // STEP,),
-        in_specs=[smem, *x_specs(), pl.BlockSpec(memory_space=pl.ANY)],
+        in_specs=[
+            smem,
+            pl.BlockSpec((16, 2, 2, STEP * 8, 128), lambda i: (0, 0, 0, i, 0)),
+            *FACTORS,
+            pl.BlockSpec(memory_space=pl.ANY),
+        ],
         out_specs=pl.BlockSpec((2, STEP, 64, GRID), lambda i: (0, ROWS_A // STEP + i, 0, 0)),
         out_shape=OUT_SHAPE,
-        input_output_aliases={4: 0},
+        scratch_shapes=TABLES,
+        input_output_aliases={6: 0},
+        compiler_params=pltpu.CompilerParams(vmem_limit_bytes=24 * 2**20),
         name="x_stage_b",
         cost_estimate=pl.CostEstimate(flops=4 * 10**9, bytes_accessed=6 * 10**6, transcendentals=0),
-    )(side, blocks, *tables, whole)
-
-
-def pair_groups():
-    ids = np.arange(256).reshape(32, 8)
-    return [
-        np.stack([ids[:, q], ids[:, 7 - q]], axis=1).reshape(-1).tolist() for q in range(4)
-    ]
-
-
-def exchange(blocks, rows):
-    blocks = blocks.reshape(64, rows * 8, 128)
-    blocks = lax.all_to_all(
-        blocks, ALL, split_axis=0, concat_axis=0, tiled=True, axis_index_groups=pair_groups()
+    )(side, blocks, *x_factors(), whole)
+
+
+def pair_groups(split_cores):
+    ids = np.arange(256).reshape(16, 2, 8)
+    groups = []
+    for q in range(4):
+        members = np.stack([ids[:, :, q], ids[:, :, 7 - q]], axis=2)
+        if split_cores:
+            groups += [members[:, core].reshape(-1).tolist() for core in range(2)]
+        else:
+            groups.append(members.reshape(-1).tolist())
+    return groups
+
+
+def exchange(blocks, split_cores):
+    return lax.all_to_all(
+        blocks, ALL, split_axis=0, concat_axis=0, tiled=True, axis_index_groups=pair_groups(split_cores)
     )
-    return blocks.reshape(32, 2, rows * 8, 128)
 
 
 def all_sum(value):
-    for axis in (("px_2",), ("px_0",), ("py_1",), ("px_1", "py_0")):
+    for axis in (("px_2",), ("px_0",), ("py_1",), ("px_1",), ("py_0",)):
         size = lax.axis_size(axis)
         parts = [value]
         for k in range(1, size):
@@ -429,17 +557,21 @@
     col_numbers = lax.dynamic_slice_in_dim(numbers, col_position * 64, 64, axis=1).T
     y_numbers = lax.dynamic_slice_in_dim(numbers, row_position * 16, 16, axis=1)
 
-    (part_a,) = y_stage(planes, range(ROWS_A), False)
-    part_a = exchange(part_a, ROWS_A)
+    part_a, planes = y_stage_a(planes)
+    part_a = exchange(part_a, False).reshape(32, 2, ROWS_A * 8, 128)
     planes, numbers, col_numbers, y_numbers = lax.optimization_barrier(
         (planes, numbers, col_numbers, y_numbers)
     )
-    part_b, *tables_x = y_stage(planes, range(ROWS_A, 16), True)
-    part_b = exchange(part_b, ROWS_B)
-
-    whole, sums = x_stage_a(side.reshape(1), y_numbers, part_a, tables_x, numbers, col_numbers)
+    core = lax.axis_index("px_2")
+    keep, send = y_stage_b(core.reshape(1), planes)
+    received = lax.ppermute(send, "px_2", [(0, 1), (1, 0)])
+    lower = core == 0
+    halves_of_x = [jnp.where(lower, keep, received), jnp.where(lower, received, keep)]
+    part_b = exchange(jnp.stack(halves_of_x, axis=1), True).reshape(16, 2, 2, ROWS_B * 8, 128)
+
+    whole, sums = x_stage_a(side.reshape(1), y_numbers, part_a, numbers, col_numbers)
     sums = all_sum(sums).sum(axis=1)
-    structure = x_stage_b(side.reshape(1), part_b, tables_x, whole)
+    structure = x_stage_b(side.reshape(1), part_b, whole)
     energy = 0.5 * sums[0]
     virial = energy * jnp.array([1.0, 1.0, 1.0, 0.0, 0.0, 0.0], dtype=f32) - sums[1:7]
     return structure, energy, virial

time: 182 us -> 177 us (0.973)
  starting transfers between devices: 41.1 us -> 34.7 us
  waiting for transfers between devices: 67.1 us -> 72.7 us
  Pallas kernels: 31.6 us -> 26.8 us
    ppermute x14 -> x11, starting transfers between devices: 22.9 us -> 17.2 us  [all_sum(): parts.append(lax.ppermute(value, axis, [(s, s ^ k) for s in range(size)]))]
    ppermute x14 -> x11, waiting for transfers between devices: 11.1 us -> 15.9 us  [all_sum(): parts.append(lax.ppermute(value, axis, [(s, s ^ k) for s in range(size)]))]
    pallas_call x3, Pallas kernels: 17 us -> 14.1 us  [the longest x1 4.76 us: x_stage_b(): pl.pallas_call(x_kernel_b, grid=(ROWS_B // STEP,), in_specs=[smem, pl.Blo...]
    ppermute x0 -> x1, waiting for transfers between devices: none -> 2.25 us  [body(): received = lax.ppermute(send, 'px_2', [(0, 1), (1, 0)])]
  transfers between devices with their start and end apart: 16 -> 14, of which waited for: 8 -> 10; matrix products, arithmetic and copies ran while one was open for 2% -> 2% of each run, Pallas kernels for 10% -> 10%
where the time goes in v1:
time: 177 us; the launch traced here: 176 us
  waiting for transfers between devices  72.7 us (41%)
  blocking collectives  35.2 us (20%)
  starting transfers between devices  34.7 us (20%)
  Pallas kernels  26.8 us (15%)
  other arithmetic  2.38 us (1%)
  local copies, waits for them, and re-layouts  2.16 us (1%)
  between operations  2.01 us (1%)
    all_to_all x2, waiting for transfers between devices, exchange(): lax.all_to_all(blocks, ALL, split_axis=0, concat_axis=0, tiled=True, axis...  54.6 us
    all_to_all x1, blocking collectives, body(): lax.all_to_all(planes, FIRST, split_axis=0, concat_axis=0, tiled=True)  35.2 us
    ppermute x11, starting transfers between devices, all_sum(): parts.append(lax.ppermute(value, axis, [(s, s ^ k) for s in range(size)]))  17.2 us
    all_to_all x2, starting transfers between devices, exchange(): lax.all_to_all(blocks, ALL, split_axis=0, concat_axis=0, tiled=True, axis...  17 us
    ppermute x11, waiting for transfers between devices, all_sum(): parts.append(lax.ppermute(value, axis, [(s, s ^ k) for s in range(size)]))  15.9 us
    pallas_call x1, Pallas kernels, x_stage_a(): pl.pallas_call(x_kernel_a, grid=(ROWS_A // STEP,), in_specs=[smem, smem,...  7.38 us
    pallas_call x1, Pallas kernels, z_stage(): pl.pallas_call(z_kernel, grid=(4,), in_specs=[pl.BlockSpec((8, 32, GRID),...  5.31 us
    pallas_call x1, Pallas kernels, x_stage_b(): pl.pallas_call(x_kernel_b, grid=(ROWS_B // STEP,), in_specs=[smem, pl.Blo...  4.76 us
  transfers between devices with their start and end apart: 14, of which 10 were waited for; matrix products, arithmetic and copies ran while one was open for 2% of the time, Pallas kernels for 10%

profile of v1, /device:TPU:1, one launch (start us, length us, event | category | flops | bytes accessed | tf_op | source)
XLA Modules:
  0.0 176.0 jit_solution(16712704257674417878)
XLA Ops:
  0.6 5.3 %z_stage.1 = f32[16,264,128]{2,1,0:T(8,128)S(1)} custom-call(f32[32,32,512]{2,1,0:T(8,128)} %bitcast.17, bf16[512,640]{1,0:T(8,128)(2,1)} %constant.63.clone.high_ref, bf16[512,640]{1,0:T(8,128)(2,1)} %constant.64.clone.low_ref), custom_call_target="tpu_custom_call" | custom-call | flops 4000000000 | bytes 6000000 | tf_op jit(solution)/shard_map/z_stage/pallas_call | solution.py:124
  6.0 35.2 %all_to_all.15.refs_0_ = f32[16,264,128]{2,1,0:T(8,128)S(1)} all-to-all(f32[16,264,128]{2,1,0:T(8,128)S(1)} %z_stage.1), channel_id=1, replica_groups=mesh['px_0'=4,'px_1'=4,'px_2'=2,'py_0'=2,'py_1'=4] {'px_2','py_0','py_1'}, dimensions={0} | all-to-all | bytes 4325376 | tf_op jit(solution)/shard_map/all_to_all | solution.py:553
  41.2 4.6 %y_stage_a.1 = (f32[64,80,128]{2,1,0:T(8,128)}, f32[16,264,128]{2,1,0:T(8,128)}) custom-call(f32[16,264,128]{2,1,0:T(8,128)S(1)} %all_to_all.15.refs_0_, f32[32,256]{1,0:T(8,128)S(1)} %copy-done.2, f32[32,256]{1,0:T(8,128)S(1)} %copy-done.3, f32[16,256]{1,0:T(8,128)S(1)} %copy-done.6, f32[16,256]{1,0:T(8,128)S(1)} %copy-done.7), custom_call_target="tpu_custom_call" | custom-call | flops 4000000000 | bytes 6000000 | tf_op jit(solution)/shard_map/y_stage_a/pallas_call | solution.py:274
  45.9 11.3 %all-to-all-start.2 = ((f32[64,80,128]{2,1,0:T(8,128)}), f32[64,80,128]{2,1,0:T(8,128)S(1)}, u32[]{:S(2)}, u32[]{:S(2)}) async-start(f32[64,80,128]{2,1,0:T(8,128)} %get-tuple-element.18), calls=%async_computation.2 | async-start | bytes 5242880 | tf_op jit(solution)/shard_map/all_to_all | solution.py:531
  57.3 0.4 reverse.2
  58.1 4.7 %y_stage_b.1 = (f32[32,48,128]{2,1,0:T(8,128)}, f32[32,48,128]{2,1,0:T(8,128)}) custom-call(s32[1]{0:T(128)} %bitcast.1.refs_0_, f32[16,264,128]{2,1,0:T(8,128)} %get-tuple-element.14.refs_1_, f32[32,256]{1,0:T(8,128)} %constant.66.clone.refs_1_.refs_2_, f32[32,256]{1,0:T(8,128)} %constant.67.clone.refs_2_.refs_3_, ...), custom_call_target="tpu_custom_call" | custom-call | flops 4000000000 | bytes 6000000 | tf_op jit(solution)/shard_map/y_stage_b/pallas_call | solution.py:300
  62.8 0.5 collective-permute-start
  63.3 2.3 %collective-permute-done = f32[32,48,128]{2,1,0:T(8,128)} collective-permute-done((f32[32,48,128]{2,1,0:T(8,128)}, f32[32,48,128]{2,1,0:T(8,128)}, u32[]{:S(2)}, u32[]{:S(2)}) %collective-permute-start) | collective-permute-done | bytes 786464 | tf_op jit(solution)/shard_map/ppermute | solution.py:567
  65.5 1.5 select_bitcast_fusion.1
  67.1 1.3 copy.33
  68.5 52.3 %all-to-all-done.2 = f32[64,80,128]{2,1,0:T(8,128)S(1)} async-done(((f32[64,80,128]{2,1,0:T(8,128)}), f32[64,80,128]{2,1,0:T(8,128)S(1)}, u32[]{:S(2)}, u32[]{:S(2)}) %all-to-all-start.2) | async-done | bytes 2621472 | tf_op jit(solution)/shard_map/all_to_all | solution.py:531
  120.7 5.7 %all-to-all-start.1 = ((f32[32,2,48,128]{3,2,1,0:T(8,128)}), f32[32,2,48,128]{3,2,1,0:T(8,128)}, u32[]{:S(2)}, u32[]{:S(2)}) async-start(f32[32,2,48,128]{3,2,1,0:T(8,128)} %copy.33), calls=%async_computation.1 | async-start | bytes 3145728 | tf_op jit(solution)/shard_map/all_to_all | solution.py:531
  126.5 7.4 %x_stage_a.1 = (f32[2,16,64,512]{3,2,1,0:T(8,128)}, f32[8,128]{1,0:T(8,128)S(1)}) custom-call(s32[1]{0:T(128)} %bitcast.side_ref, f32[10,16]{1,0:T(8,128)S(1)} %constant_dynamic-slice_fusion.y_ref, f32[32,2,80,128]{3,2,1,0:T(8,128)S(1)} %bitcast.13, f32[16,256]{1,0:T(8,128)S(1)} %copy-done.4, f32[16,256]{1,0:T(8,128)S(1)} %copy-done.5, ...), custom_call_target="tpu_custom_call" | custom-call | flops 4000000000 | bytes 6000000 | tf_op jit(solution)/shard_map/x_stage_a/pallas_call | solution.py:474
  133.8 1.2 collective-permute-start.1
  135.1 0.8 collective-permute-done.1
  135.9 1.4 collective-permute-start.2
  137.3 2.4 %collective-permute-start.3 = (f32[8,128]{1,0:T(8,128)S(1)}, f32[8,128]{1,0:T(8,128)S(1)}, u32[]{:S(2)}, u32[]{:S(2)}) collective-permute-start(f32[8,128]{1,0:T(8,128)S(1)} %add.53), channel_id=1, source_target_pairs={{0,128},{64,192},{128,0},{192,64},{1,129},{65,193},{129,1},{193,65... | collective-permute-start | bytes 12296 | tf_op jit(solution)/shard_map/ppermute | solution.py:541
  139.8 1.9 %collective-permute-done.3 = f32[8,128]{1,0:T(8,128)S(1)} collective-permute-done((f32[8,128]{1,0:T(8,128)S(1)}, f32[8,128]{1,0:T(8,128)S(1)}, u32[]{:S(2)}, u32[]{:S(2)}) %collective-permute-start.3) | collective-permute-done | bytes 4128 | tf_op jit(solution)/shard_map/ppermute | solution.py:541
  141.7 2.2 %collective-permute-done.4 = f32[8,128]{1,0:T(8,128)S(1)} collective-permute-done((f32[8,128]{1,0:T(8,128)S(1)}, f32[8,128]{1,0:T(8,128)S(1)}, u32[]{:S(2)}, u32[]{:S(2)}) %collective-permute-start.4) | collective-permute-done | bytes 4128 | tf_op jit(solution)/shard_map/ppermute | solution.py:541
  143.9 2.7 %collective-permute-start.6 = (f32[8,128]{1,0:T(8,128)S(1)}, f32[8,128]{1,0:T(8,128)S(1)}, u32[]{:S(2)}, u32[]{:S(2)}) collective-permute-start(f32[8,128]{1,0:T(8,128)S(1)} %add_add_fusion.2), channel_id=1, source_target_pairs={{0,2},{1,3},{2,0},{3,1},{4,6},{5,7},{6,4},{7,5},{8,10},{9,11},{10,... | collective-permute-start | bytes 12296 | tf_op jit(solution)/shard_map/ppermute | solution.py:541
  146.6 1.1 collective-permute-start.7
  147.7 0.8 collective-permute-done.6
  148.5 2.6 %collective-permute-done.7 = f32[8,128]{1,0:T(8,128)S(1)} collective-permute-done((f32[8,128]{1,0:T(8,128)S(1)}, f32[8,128]{1,0:T(8,128)S(1)}, u32[]{:S(2)}, u32[]{:S(2)}) %collective-permute-start.7) | collective-permute-done | bytes 4128 | tf_op jit(solution)/shard_map/ppermute | solution.py:541
  151.1 3.1 %collective-permute-start.10 = (f32[8,128]{1,0:T(8,128)S(1)}, f32[8,128]{1,0:T(8,128)S(1)}, u32[]{:S(2)}, u32[]{:S(2)}) collective-permute-start(f32[8,128]{1,0:T(8,128)S(1)} %add_add_fusion.1), channel_id=1, source_target_pairs={{0,48},{16,32},{32,16},{48,0},{1,49},{17,33},{33,17},{49,1},{2,50}... | collective-permute-start | bytes 12296 | tf_op jit(solution)/shard_map/ppermute | solution.py:541
  154.2 1.7 collective-permute-start.8
  155.9 0.8 collective-permute-start.9
  156.8 1.3 collective-permute-done.8
  158.1 6.3 %collective-permute-done.9 = f32[8,128]{1,0:T(8,128)S(1)} collective-permute-done((f32[8,128]{1,0:T(8,128)S(1)}, f32[8,128]{1,0:T(8,128)S(1)}, u32[]{:S(2)}, u32[]{:S(2)}) %collective-permute-start.9) | collective-permute-done | bytes 4128 | tf_op jit(solution)/shard_map/ppermute | solution.py:541
  164.4 2.6 %collective-permute-start.11 = (f32[8,128]{1,0:T(8,128)S(1)}, f32[8,128]{1,0:T(8,128)S(1)}, u32[]{:S(2)}, u32[]{:S(2)}) collective-permute-start(f32[8,128]{1,0:T(8,128)S(1)} %add_add_fusion), channel_id=1, source_target_pairs={{0,4},{4,0},{1,5},{5,1},{2,6},{6,2},{3,7},{7,3},{8,12},{12,8},{9,1... | collective-permute-start | bytes 12296 | tf_op jit(solution)/shard_map/ppermute | solution.py:541
  167.0 2.3 %all-to-all-done.1 = f32[32,2,48,128]{3,2,1,0:T(8,128)} async-done(((f32[32,2,48,128]{3,2,1,0:T(8,128)}), f32[32,2,48,128]{3,2,1,0:T(8,128)}, u32[]{:S(2)}, u32[]{:S(2)}) %all-to-all-start.1) | async-done | bytes 1572896 | tf_op jit(solution)/shard_map/all_to_all | solution.py:531
  169.3 4.8 %x_stage_b.1 = f32[2,16,64,512]{3,2,1,0:T(8,128)} custom-call(s32[1]{0:T(128)} %bitcast.side_ref, f32[16,2,2,48,128]{4,3,2,1,0:T(8,128)} %bitcast.6.g_ref, f32[16,256]{1,0:T(8,128)S(1)} %copy-done.4, f32[16,256]{1,0:T(8,128)S(1)} %copy-done.5, f32[32,256]{1,0:T(8,128)S(1)} %copy-done, f32[32,256]{1,0:T(8,128)S(1)} %copy-done.1, ...), custom_call_target="tpu_custom_call", output_to_operand_aliasing={{}: (6, {})} | custom-call | flops 4000000000 | bytes 6000000 | tf_op jit(solution)/shard_map/x_stage_b/pallas_call | solution.py:499
  174.3 0.6 slice_subtract_fusion
  (42 shorter events, 0.8 us)
Async XLA Ops:
  6.0 35.3 %copy-start.2 = (f32[32,256]{1,0:T(8,128)S(1)}, f32[32,256]{1,0:T(8,128)}, u32[]{:S(2)}) copy-start(f32[32,256]{1,0:T(8,128)} %constant.66.clone.refs_1_.refs_2_) | copy-start | bytes 98308
  6.0 35.2 %copy-start.3 = (f32[32,256]{1,0:T(8,128)S(1)}, f32[32,256]{1,0:T(8,128)}, u32[]{:S(2)}) copy-start(f32[32,256]{1,0:T(8,128)} %constant.67.clone.refs_2_.refs_3_) | copy-start | bytes 98308
  6.0 35.2 %copy-start.6 = (f32[16,256]{1,0:T(8,128)S(1)}, f32[16,256]{1,0:T(8,128)}, u32[]{:S(2)}) copy-start(f32[16,256]{1,0:T(8,128)} %constant.68.clone.refs_3_.refs_4_) | copy-start | bytes 49156
  6.0 35.2 %copy-start.7 = (f32[16,256]{1,0:T(8,128)S(1)}, f32[16,256]{1,0:T(8,128)}, u32[]{:S(2)}) copy-start(f32[16,256]{1,0:T(8,128)} %constant.69.clone.refs_4_.refs_5_) | copy-start | bytes 49156
  45.8 11.4 %copy-start.8 = (f32[3,512]{1,0:T(4,128)S(1)}, f32[3,512]{1,0:T(4,128)}, u32[]{:S(2)}) copy-start(f32[3,512]{1,0:T(4,128)} %param.23) | copy-start | bytes 18436
  45.9 11.9 %slice-start = ((f32[3,512]{1,0:T(4,128)}), f32[3,1]{1,0:T(4,128)S(1)}, s32[]{:S(2)}) async-start(f32[3,512]{1,0:T(4,128)} %param.23), calls=%async_computation.3 | async-start | bytes 4096 | tf_op jit(solution)/shard_map/jit(_roll_static)/slice | solution.py:555
  45.9 11.9 %copy-start.9 = (f32[4,512]{1,0:T(4,128)S(1)}, f32[4,512]{1,0:T(4,128)}, u32[]{:S(2)}) copy-start(f32[4,512]{1,0:T(4,128)} %constant.65.clone) | copy-start | bytes 24580
  45.9 74.8 %all-to-all-start.2 = ((f32[64,80,128]{2,1,0:T(8,128)}), f32[64,80,128]{2,1,0:T(8,128)S(1)}, u32[]{:S(2)}, u32[]{:S(2)}) async-start(f32[64,80,128]{2,1,0:T(8,128)} %get-tuple-element.18), calls=%async_computation.2 | async-start | bytes 5242880 | tf_op jit(solution)/shard_map/all_to_all | solution.py:531
  62.8 2.7 %collective-permute-start = (f32[32,48,128]{2,1,0:T(8,128)}, f32[32,48,128]{2,1,0:T(8,128)}, u32[]{:S(2)}, u32[]{:S(2)}) collective-permute-start(f32[32,48,128]{2,1,0:T(8,128)} %get-tuple-element.16), channel_id=1, source_target_pairs={{0,8},{8,0},{1,9},{9,1},{2,10},{10,2},{3,11},{11,3},{4,12},{12,4},... | collective-permute-start | bytes 2359304 | tf_op jit(solution)/shard_map/ppermute | solution.py:567
  68.4 58.0 %copy-start = (f32[32,256]{1,0:T(8,128)S(1)}, f32[32,256]{1,0:T(8,128)}, u32[]{:S(2)}) copy-start(f32[32,256]{1,0:T(8,128)} %constant.72.clone.bc_ref) | copy-start | bytes 98308
  68.4 58.0 %copy-start.1 = (f32[32,256]{1,0:T(8,128)S(1)}, f32[32,256]{1,0:T(8,128)}, u32[]{:S(2)}) copy-start(f32[32,256]{1,0:T(8,128)} %constant.73.clone.bs_ref) | copy-start | bytes 98308
  68.4 58.0 %copy-start.4 = (f32[16,256]{1,0:T(8,128)S(1)}, f32[16,256]{1,0:T(8,128)}, u32[]{:S(2)}) copy-start(f32[16,256]{1,0:T(8,128)} %constant.70.clone.ac_ref) | copy-start | bytes 49156
  68.4 58.0 %copy-start.5 = (f32[16,256]{1,0:T(8,128)S(1)}, f32[16,256]{1,0:T(8,128)}, u32[]{:S(2)}) copy-start(f32[16,256]{1,0:T(8,128)} %constant.71.clone.as_ref) | copy-start | bytes 49156
  120.7 48.6 %all-to-all-start.1 = ((f32[32,2,48,128]{3,2,1,0:T(8,128)}), f32[32,2,48,128]{3,2,1,0:T(8,128)}, u32[]{:S(2)}, u32[]{:S(2)}) async-start(f32[32,2,48,128]{3,2,1,0:T(8,128)} %copy.33), calls=%async_computation.1 | async-start | bytes 3145728 | tf_op jit(solution)/shard_map/all_to_all | solution.py:531
  133.8 2.0 %collective-permute-start.1 = (f32[8,128]{1,0:T(8,128)S(1)}, f32[8,128]{1,0:T(8,128)S(1)}, u32[]{:S(2)}, u32[]{:S(2)}) collective-permute-start(f32[8,128]{1,0:T(8,128)S(1)} %get-tuple-element.22), channel_id=1, source_target_pairs={{0,8},{8,0},{1,9},{9,1},{2,10},{10,2},{3,11},{11,3},{4,12},{12,4},... | collective-permute-start | bytes 12296 | tf_op jit(solution)/shard_map/ppermute | solution.py:541
  135.9 3.9 %collective-permute-start.2 = (f32[8,128]{1,0:T(8,128)S(1)}, f32[8,128]{1,0:T(8,128)S(1)}, u32[]{:S(2)}, u32[]{:S(2)}) collective-permute-start(f32[8,128]{1,0:T(8,128)S(1)} %add.53), channel_id=1, source_target_pairs={{0,64},{64,0},{128,192},{192,128},{1,65},{65,1},{129,193},{193,129... | collective-permute-start | bytes 12296 | tf_op jit(solution)/shard_map/ppermute | solution.py:541
  137.3 4.4 %collective-permute-start.3 = (f32[8,128]{1,0:T(8,128)S(1)}, f32[8,128]{1,0:T(8,128)S(1)}, u32[]{:S(2)}, u32[]{:S(2)}) collective-permute-start(f32[8,128]{1,0:T(8,128)S(1)} %add.53), channel_id=1, source_target_pairs={{0,128},{64,192},{128,0},{192,64},{1,129},{65,193},{129,1},{193,65... | collective-permute-start | bytes 12296 | tf_op jit(solution)/shard_map/ppermute | solution.py:541
  139.8 4.1 %collective-permute-start.4 = (f32[8,128]{1,0:T(8,128)S(1)}, f32[8,128]{1,0:T(8,128)S(1)}, u32[]{:S(2)}, u32[]{:S(2)}) collective-permute-start(f32[8,128]{1,0:T(8,128)S(1)} %add.53), channel_id=1, source_target_pairs={{0,192},{64,128},{128,64},{192,0},{1,193},{65,129},{129,65},{193,1... | collective-permute-start | bytes 12296 | tf_op jit(solution)/shard_map/ppermute | solution.py:541
  143.9 3.9 %collective-permute-start.5 = (f32[8,128]{1,0:T(8,128)S(1)}, f32[8,128]{1,0:T(8,128)S(1)}, u32[]{:S(2)}, u32[]{:S(2)}) collective-permute-start(f32[8,128]{1,0:T(8,128)S(1)} %add_add_fusion.2), channel_id=1, source_target_pairs={{0,1},{1,0},{2,3},{3,2},{4,5},{5,4},{6,7},{7,6},{8,9},{9,8},{10,11... | collective-permute-start | bytes 12296 | tf_op jit(solution)/shard_map/ppermute | solution.py:541
  143.9 4.6 %collective-permute-start.6 = (f32[8,128]{1,0:T(8,128)S(1)}, f32[8,128]{1,0:T(8,128)S(1)}, u32[]{:S(2)}, u32[]{:S(2)}) collective-permute-start(f32[8,128]{1,0:T(8,128)S(1)} %add_add_fusion.2), channel_id=1, source_target_pairs={{0,2},{1,3},{2,0},{3,1},{4,6},{5,7},{6,4},{7,5},{8,10},{9,11},{10,... | collective-permute-start | bytes 12296 | tf_op jit(solution)/shard_map/ppermute | solution.py:541
  146.6 4.5 %collective-permute-start.7 = (f32[8,128]{1,0:T(8,128)S(1)}, f32[8,128]{1,0:T(8,128)S(1)}, u32[]{:S(2)}, u32[]{:S(2)}) collective-permute-start(f32[8,128]{1,0:T(8,128)S(1)} %add_add_fusion.2), channel_id=1, source_target_pairs={{0,3},{1,2},{2,1},{3,0},{4,7},{5,6},{6,5},{7,4},{8,11},{9,10},{10,... | collective-permute-start | bytes 12296 | tf_op jit(solution)/shard_map/ppermute | solution.py:541
  151.1 5.7 %collective-permute-start.10 = (f32[8,128]{1,0:T(8,128)S(1)}, f32[8,128]{1,0:T(8,128)S(1)}, u32[]{:S(2)}, u32[]{:S(2)}) collective-permute-start(f32[8,128]{1,0:T(8,128)S(1)} %add_add_fusion.1), channel_id=1, source_target_pairs={{0,48},{16,32},{32,16},{48,0},{1,49},{17,33},{33,17},{49,1},{2,50}... | collective-permute-start | bytes 12296 | tf_op jit(solution)/shard_map/ppermute | solution.py:541
  154.2 3.9 %collective-permute-start.8 = (f32[8,128]{1,0:T(8,128)S(1)}, f32[8,128]{1,0:T(8,128)S(1)}, u32[]{:S(2)}, u32[]{:S(2)}) collective-permute-start(f32[8,128]{1,0:T(8,128)S(1)} %add_add_fusion.1), channel_id=1, source_target_pairs={{0,16},{16,0},{32,48},{48,32},{1,17},{17,1},{33,49},{49,33},{2,18}... | collective-permute-start | bytes 12296 | tf_op jit(solution)/shard_map/ppermute | solution.py:541
  155.9 8.5 %collective-permute-start.9 = (f32[8,128]{1,0:T(8,128)S(1)}, f32[8,128]{1,0:T(8,128)S(1)}, u32[]{:S(2)}, u32[]{:S(2)}) collective-permute-start(f32[8,128]{1,0:T(8,128)S(1)} %add_add_fusion.1), channel_id=1, source_target_pairs={{0,32},{16,48},{32,0},{48,16},{1,33},{17,49},{33,1},{49,17},{2,34}... | collective-permute-start | bytes 12296 | tf_op jit(solution)/shard_map/ppermute | solution.py:541
  164.4 9.7 %collective-permute-start.11 = (f32[8,128]{1,0:T(8,128)S(1)}, f32[8,128]{1,0:T(8,128)S(1)}, u32[]{:S(2)}, u32[]{:S(2)}) collective-permute-start(f32[8,128]{1,0:T(8,128)S(1)} %add_add_fusion), channel_id=1, source_target_pairs={{0,4},{4,0},{1,5},{5,1},{2,6},{6,2},{3,7},{7,3},{8,12},{12,8},{9,1... | collective-permute-start | bytes 12296 | tf_op jit(solution)/shard_map/ppermute | solution.py:541
  169.3 4.9 %copy-start.10 = (f32[6]{0:T(128)S(1)}, f32[6]{0:T(128)}, u32[]{:S(2)}) copy-start(f32[6]{0:T(128)} %constant.74.clone) | copy-start | bytes 76

commit v2 on v1

--- a/solution.py
+++ b/solution.py
@@ -83,14 +83,14 @@
 
 def z_kernel(x_ref, high_ref, low_ref, out_ref, ext_ref):
     step = pl.program_id(0)
-    core = step // 2
-    x_high, x_low = halves(x_ref[...].reshape(256, GRID))
+    core = step // 1
+    x_high, x_low = halves(x_ref[...].reshape(512, GRID))
     w_high = high_ref[...]
     result = dot(x_high, w_high) + dot(x_low, w_high) + dot(x_high, low_ref[...])
     low_lanes = lane_index((32, 128)) < 64
     lane = lane_index((8, 128))
-    for k in range(4):
-        row = pl.multiple_of((step % 2) * 128 + k * 32, 32)
+    for k in range(8):
+        row = pl.multiple_of((step % 1) * 256 + k * 32, 32)
         even = result[k * 64 : k * 64 + 32]
         odd = result[k * 64 + 32 : k * 64 + 64]
         for t in range(4):
@@ -107,9 +107,9 @@
                 piece = result[start : start + 8, 512:]
                 here = (lane // 64 == parity) & (lane // 8 % 4 == quarter)
                 extra = jnp.where(here, piece, extra)
-        ext_ref[step * 4 + k] = extra
-
-    @pl.when(step == 3)
+        ext_ref[step * 8 + k] = extra
+
+    @pl.when(step == 1)
     def _():
         for c in range(2):
             for h in range(8):
@@ -123,9 +123,9 @@
 def z_stage(block, tables):
     return pl.pallas_call(
         z_kernel,
-        grid=(4,),
+        grid=(2,),
         in_specs=[
-            pl.BlockSpec((8, 32, GRID), lambda i: (i, 0, 0)),
+            pl.BlockSpec((16, 32, GRID), lambda i: (i, 0, 0)),
             pl.BlockSpec((GRID, 640), lambda i: (0, 0)),
             pl.BlockSpec((GRID, 640), lambda i: (0, 0)),
         ],
@@ -229,11 +229,12 @@
         return carry
 
     def deliver(part):
-        lax.fori_loop(part * 16, part * 16 + 16, gather, 0)
-        flush(part).start()
+        for half in range(2):
+            lax.fori_loop(half * 16, half * 16 + 16, gather, 0)
+            flush(half).start()
 
     factors = (pc_ref, ps_ref, oc_ref, os_ref)
-    y_rows(offsets, 2, g_ref, factors, stage_ref, lambda *_: None, deliver)
+    y_rows(offsets, 1, g_ref, factors, stage_ref, lambda *_: None, deliver)
     copy.wait()
     flush(0).wait()
     flush(1).wait()
@@ -281,7 +282,7 @@
         ],
         scratch_shapes=[
             pltpu.VMEM((64, rows * 8, 128), f32),
-            pltpu.VMEM((8 * (rows * 64 + 8), 128), f32),
+            pltpu.VMEM((9 * (rows * 64 + 8), 128), f32),
             pltpu.SemaphoreType.DMA,
             pltpu.SemaphoreType.DMA((2,)),
         ],
@@ -302,7 +303,7 @@
         in_specs=[pl.BlockSpec(memory_space=pltpu.SMEM)] + [WHOLE] * 5,
         out_specs=[WHOLE, WHOLE],
         out_shape=[jax.ShapeDtypeStruct((32, rows * 8, 128), f32)] * 2,
-        scratch_shapes=[pltpu.VMEM((8 * (rows * 64 + 8), 128), f32)],
+        scratch_shapes=[pltpu.VMEM((9 * (rows * 64 + 8), 128), f32)],
         name="y_stage_b",
         cost_estimate=pl.CostEstimate(flops=4 * 10**9, bytes_accessed=6 * 10**6, transcendentals=0),
     )(core, blocks, *y_factors())
@@ -338,7 +339,7 @@
         scratch_shapes=[
             pltpu.VMEM((16, EXT, 128), f32),
             pltpu.VMEM((64, rows * 8, 128), f32),
-            pltpu.VMEM((8 * (rows * 64 + 8), 128), f32),
+            pltpu.VMEM((9 * (rows * 64 + 8), 128), f32),
             pltpu.SemaphoreType.DMA((5,)),
             pltpu.SemaphoreType.DMA((4,)),
         ],
@@ -450,7 +451,11 @@
     def _():
         total = acc_ref[...]
         total = total[:, :, :128] + total[:, :, 128:256] + total[:, :, 256:384] + total[:, :, 384:]
-        sum_ref[0:7, :] = total.sum(axis=1)
+        totals = jnp.sum(total.sum(axis=1), axis=1, keepdims=True)
+        energy = 0.5 * totals[0:1]
+        sum_ref[0:1, :] = jnp.broadcast_to(energy, (1, 128))
+        sum_ref[1:4, :] = jnp.broadcast_to(energy - totals[1:4], (3, 128))
+        sum_ref[4:7, :] = jnp.broadcast_to(-totals[4:7], (3, 128))
         sum_ref[7:8, :] = jnp.zeros((1, 128), f32)
 
 
@@ -570,11 +575,9 @@
     part_b = exchange(jnp.stack(halves_of_x, axis=1), True).reshape(16, 2, 2, ROWS_B * 8, 128)
 
     whole, sums = x_stage_a(side.reshape(1), y_numbers, part_a, numbers, col_numbers)
-    sums = all_sum(sums).sum(axis=1)
+    sums = all_sum(sums)
     structure = x_stage_b(side.reshape(1), part_b, whole)
-    energy = 0.5 * sums[0]
-    virial = energy * jnp.array([1.0, 1.0, 1.0, 0.0, 0.0, 0.0], dtype=f32) - sums[1:7]
-    return structure, energy, virial
+    return structure, sums[0, 0], sums[1:7, 0]
 
 
 def solution(mesh):

time: 177 us -> 175 us (0.989)
  no operation moved by 1% of the time
where the time goes in v2:
time: 175 us; the launch traced here: 174 us
  waiting for transfers between devices  72.6 us (41%)
  blocking collectives  35.2 us (20%)
  starting transfers between devices  34.7 us (20%)
  Pallas kernels  25.7 us (15%)
  local copies, waits for them, and re-layouts  3.3 us (2%)
    all_to_all x2, waiting for transfers between devices, exchange(): lax.all_to_all(blocks, ALL, split_axis=0, concat_axis=0, tiled=True, axis...  54.6 us
    all_to_all x1, blocking collectives, body(): lax.all_to_all(planes, FIRST, split_axis=0, concat_axis=0, tiled=True)  35.2 us
    ppermute x11, starting transfers between devices, all_sum(): parts.append(lax.ppermute(value, axis, [(s, s ^ k) for s in range(size)]))  17.2 us
    all_to_all x2, starting transfers between devices, exchange(): lax.all_to_all(blocks, ALL, split_axis=0, concat_axis=0, tiled=True, axis...  17 us
    ppermute x11, waiting for transfers between devices, all_sum(): parts.append(lax.ppermute(value, axis, [(s, s ^ k) for s in range(size)]))  15.8 us
    pallas_call x1, Pallas kernels, x_stage_a(): pl.pallas_call(x_kernel_a, grid=(ROWS_A // STEP,), in_specs=[smem, smem,...  7.46 us
    pallas_call x1, Pallas kernels, z_stage(): pl.pallas_call(z_kernel, grid=(2,), in_specs=[pl.BlockSpec((16, 32, GRID)...  4.8 us
    pallas_call x1, Pallas kernels, x_stage_b(): pl.pallas_call(x_kernel_b, grid=(ROWS_B // STEP,), in_specs=[smem, pl.Blo...  4.74 us
  transfers between devices with their start and end apart: 14, of which 10 were waited for; matrix products, arithmetic and copies ran while one was open for 2% of the time, Pallas kernels for 10%

profile of v2, /device:TPU:1, one launch (start us, length us, event | category | flops | bytes accessed | tf_op | source)
XLA Modules:
  0.0 174.0 jit_solution(10471370276120465170)
XLA Ops:
  0.6 4.8 %z_stage.1 = f32[16,264,128]{2,1,0:T(8,128)S(1)} custom-call(f32[32,32,512]{2,1,0:T(8,128)} %bitcast.15, bf16[512,640]{1,0:T(8,128)(2,1)} %constant.56.clone.high_ref, bf16[512,640]{1,0:T(8,128)(2,1)} %constant.57.clone.low_ref), custom_call_target="tpu_custom_call" | custom-call | flops 4000000000 | bytes 6000000 | tf_op jit(solution)/shard_map/z_stage/pallas_call | solution.py:124
  5.5 35.2 %all_to_all.15.refs_0_ = f32[16,264,128]{2,1,0:T(8,128)S(1)} all-to-all(f32[16,264,128]{2,1,0:T(8,128)S(1)} %z_stage.1), channel_id=1, replica_groups=mesh['px_0'=4,'px_1'=4,'px_2'=2,'py_0'=2,'py_1'=4] {'px_2','py_0','py_1'}, dimensions={0} | all-to-all | bytes 4325376 | tf_op jit(solution)/shard_map/all_to_all | solution.py:558
  40.7 4.0 %y_stage_a.1 = (f32[64,80,128]{2,1,0:T(8,128)}, f32[16,264,128]{2,1,0:T(8,128)}) custom-call(f32[16,264,128]{2,1,0:T(8,128)S(1)} %all_to_all.15.refs_0_, f32[32,256]{1,0:T(8,128)S(1)} %copy-done.2, f32[32,256]{1,0:T(8,128)S(1)} %copy-done.3, f32[16,256]{1,0:T(8,128)S(1)} %copy-done.6, f32[16,256]{1,0:T(8,128)S(1)} %copy-done.7), custom_call_target="tpu_custom_call" | custom-call | flops 4000000000 | bytes 6000000 | tf_op jit(solution)/shard_map/y_stage_a/pallas_call | solution.py:275
  44.7 11.3 %all-to-all-start.2 = ((f32[64,80,128]{2,1,0:T(8,128)}), f32[64,80,128]{2,1,0:T(8,128)S(1)}, u32[]{:S(2)}, u32[]{:S(2)}) async-start(f32[64,80,128]{2,1,0:T(8,128)} %get-tuple-element.18), calls=%async_computation.2 | async-start | bytes 5242880 | tf_op jit(solution)/shard_map/all_to_all | solution.py:536
  56.9 4.7 %y_stage_b.1 = (f32[32,48,128]{2,1,0:T(8,128)}, f32[32,48,128]{2,1,0:T(8,128)}) custom-call(s32[1]{0:T(128)} %bitcast.1.refs_0_, f32[16,264,128]{2,1,0:T(8,128)} %get-tuple-element.14.refs_1_, f32[32,256]{1,0:T(8,128)} %constant.59.clone.refs_1_.refs_2_, f32[32,256]{1,0:T(8,128)} %constant.60.clone.refs_2_.refs_3_, ...), custom_call_target="tpu_custom_call" | custom-call | flops 4000000000 | bytes 6000000 | tf_op jit(solution)/shard_map/y_stage_b/pallas_call | solution.py:301
  61.6 0.5 collective-permute-start
  62.1 2.3 %collective-permute-done = f32[32,48,128]{2,1,0:T(8,128)} collective-permute-done((f32[32,48,128]{2,1,0:T(8,128)}, f32[32,48,128]{2,1,0:T(8,128)}, u32[]{:S(2)}, u32[]{:S(2)}) %collective-permute-start) | collective-permute-done | bytes 786464 | tf_op jit(solution)/shard_map/ppermute | solution.py:572
  64.3 1.5 select_bitcast_fusion.1
  65.9 1.4 copy.38
  67.3 52.3 %all-to-all-done.2 = f32[64,80,128]{2,1,0:T(8,128)S(1)} async-done(((f32[64,80,128]{2,1,0:T(8,128)}), f32[64,80,128]{2,1,0:T(8,128)S(1)}, u32[]{:S(2)}, u32[]{:S(2)}) %all-to-all-start.2) | async-done | bytes 2621472 | tf_op jit(solution)/shard_map/all_to_all | solution.py:536
  119.5 5.7 %all-to-all-start.1 = ((f32[32,2,48,128]{3,2,1,0:T(8,128)}), f32[32,2,48,128]{3,2,1,0:T(8,128)}, u32[]{:S(2)}, u32[]{:S(2)}) async-start(f32[32,2,48,128]{3,2,1,0:T(8,128)} %copy.38), calls=%async_computation.1 | async-start | bytes 3145728 | tf_op jit(solution)/shard_map/all_to_all | solution.py:536
  125.3 7.5 %x_stage_a.1 = (f32[2,16,64,512]{3,2,1,0:T(8,128)}, f32[8,128]{1,0:T(8,128)S(1)}) custom-call(s32[1]{0:T(128)} %bitcast.side_ref, f32[10,16]{1,0:T(8,128)S(1)} %constant_dynamic-slice_fusion.y_ref, f32[32,2,80,128]{3,2,1,0:T(8,128)S(1)} %bitcast.12, f32[16,256]{1,0:T(8,128)S(1)} %copy-done.4, f32[16,256]{1,0:T(8,128)S(1)} %copy-done.5, ...), custom_call_target="tpu_custom_call" | custom-call | flops 4000000000 | bytes 6000000 | tf_op jit(solution)/shard_map/x_stage_a/pallas_call | solution.py:479
  132.7 1.2 collective-permute-start.1
  134.0 0.8 collective-permute-done.1
  134.8 1.4 collective-permute-start.2
  136.2 2.4 %collective-permute-start.3 = (f32[8,128]{1,0:T(8,128)S(1)}, f32[8,128]{1,0:T(8,128)S(1)}, u32[]{:S(2)}, u32[]{:S(2)}) collective-permute-start(f32[8,128]{1,0:T(8,128)S(1)} %add.53), channel_id=1, source_target_pairs={{0,128},{64,192},{128,0},{192,64},{1,129},{65,193},{129,1},{193,65... | collective-permute-start | bytes 12296 | tf_op jit(solution)/shard_map/ppermute | solution.py:546
  138.7 1.9 %collective-permute-done.3 = f32[8,128]{1,0:T(8,128)S(1)} collective-permute-done((f32[8,128]{1,0:T(8,128)S(1)}, f32[8,128]{1,0:T(8,128)S(1)}, u32[]{:S(2)}, u32[]{:S(2)}) %collective-permute-start.3) | collective-permute-done | bytes 4128 | tf_op jit(solution)/shard_map/ppermute | solution.py:546
  140.6 2.2 %collective-permute-done.4 = f32[8,128]{1,0:T(8,128)S(1)} collective-permute-done((f32[8,128]{1,0:T(8,128)S(1)}, f32[8,128]{1,0:T(8,128)S(1)}, u32[]{:S(2)}, u32[]{:S(2)}) %collective-permute-start.4) | collective-permute-done | bytes 4128 | tf_op jit(solution)/shard_map/ppermute | solution.py:546
  142.8 2.7 %collective-permute-start.6 = (f32[8,128]{1,0:T(8,128)S(1)}, f32[8,128]{1,0:T(8,128)S(1)}, u32[]{:S(2)}, u32[]{:S(2)}) collective-permute-start(f32[8,128]{1,0:T(8,128)S(1)} %add_add_fusion.2), channel_id=1, source_target_pairs={{0,2},{1,3},{2,0},{3,1},{4,6},{5,7},{6,4},{7,5},{8,10},{9,11},{10,... | collective-permute-start | bytes 12296 | tf_op jit(solution)/shard_map/ppermute | solution.py:546
  145.5 1.1 collective-permute-start.7
  146.6 0.8 collective-permute-done.6
  147.4 2.5 %collective-permute-done.7 = f32[8,128]{1,0:T(8,128)S(1)} collective-permute-done((f32[8,128]{1,0:T(8,128)S(1)}, f32[8,128]{1,0:T(8,128)S(1)}, u32[]{:S(2)}, u32[]{:S(2)}) %collective-permute-start.7) | collective-permute-done | bytes 4128 | tf_op jit(solution)/shard_map/ppermute | solution.py:546
  149.9 3.2 %collective-permute-start.10 = (f32[8,128]{1,0:T(8,128)S(1)}, f32[8,128]{1,0:T(8,128)S(1)}, u32[]{:S(2)}, u32[]{:S(2)}) collective-permute-start(f32[8,128]{1,0:T(8,128)S(1)} %add_add_fusion.1), channel_id=1, source_target_pairs={{0,48},{16,32},{32,16},{48,0},{1,49},{17,33},{33,17},{49,1},{2,50}... | collective-permute-start | bytes 12296 | tf_op jit(solution)/shard_map/ppermute | solution.py:546
  153.1 1.7 collective-permute-start.8
  154.8 0.8 collective-permute-start.9
  155.6 1.4 collective-permute-done.8
  157.0 6.3 %collective-permute-done.9 = f32[8,128]{1,0:T(8,128)S(1)} collective-permute-done((f32[8,128]{1,0:T(8,128)S(1)}, f32[8,128]{1,0:T(8,128)S(1)}, u32[]{:S(2)}, u32[]{:S(2)}) %collective-permute-start.9) | collective-permute-done | bytes 4128 | tf_op jit(solution)/shard_map/ppermute | solution.py:546
  163.2 2.6 %collective-permute-start.11 = (f32[8,128]{1,0:T(8,128)S(1)}, f32[8,128]{1,0:T(8,128)S(1)}, u32[]{:S(2)}, u32[]{:S(2)}) collective-permute-start(f32[8,128]{1,0:T(8,128)S(1)} %add_add_fusion), channel_id=1, source_target_pairs={{0,4},{4,0},{1,5},{5,1},{2,6},{6,2},{3,7},{7,3},{8,12},{12,8},{9,1... | collective-permute-start | bytes 12296 | tf_op jit(solution)/shard_map/ppermute | solution.py:546
  165.8 2.3 %all-to-all-done.1 = f32[32,2,48,128]{3,2,1,0:T(8,128)} async-done(((f32[32,2,48,128]{3,2,1,0:T(8,128)}), f32[32,2,48,128]{3,2,1,0:T(8,128)}, u32[]{:S(2)}, u32[]{:S(2)}) %all-to-all-start.1) | async-done | bytes 1572896 | tf_op jit(solution)/shard_map/all_to_all | solution.py:536
  168.1 4.7 %x_stage_b.1 = f32[2,16,64,512]{3,2,1,0:T(8,128)} custom-call(s32[1]{0:T(128)} %bitcast.side_ref, f32[16,2,2,48,128]{4,3,2,1,0:T(8,128)} %bitcast.6.g_ref, f32[16,256]{1,0:T(8,128)S(1)} %copy-done.4, f32[16,256]{1,0:T(8,128)S(1)} %copy-done.5, f32[32,256]{1,0:T(8,128)S(1)} %copy-done, f32[32,256]{1,0:T(8,128)S(1)} %copy-done.1, ...), custom_call_target="tpu_custom_call", output_to_operand_aliasing={{}: (6, {})} | custom-call | flops 4000000000 | bytes 6000000 | tf_op jit(solution)/shard_map/x_stage_b/pallas_call | solution.py:504
  172.9 0.5 slice.21
  173.4 0.6 slice_reduce_fusion
  (41 shorter events, 1.1 us)
Async XLA Ops:
  5.4 35.2 %copy-start.2 = (f32[32,256]{1,0:T(8,128)S(1)}, f32[32,256]{1,0:T(8,128)}, u32[]{:S(2)}) copy-start(f32[32,256]{1,0:T(8,128)} %constant.59.clone.refs_1_.refs_2_) | copy-start | bytes 98308
  5.4 35.2 %copy-start.3 = (f32[32,256]{1,0:T(8,128)S(1)}, f32[32,256]{1,0:T(8,128)}, u32[]{:S(2)}) copy-start(f32[32,256]{1,0:T(8,128)} %constant.60.clone.refs_2_.refs_3_) | copy-start | bytes 98308
  5.5 35.2 %copy-start.6 = (f32[16,256]{1,0:T(8,128)S(1)}, f32[16,256]{1,0:T(8,128)}, u32[]{:S(2)}) copy-start(f32[16,256]{1,0:T(8,128)} %constant.61.clone.refs_3_.refs_4_) | copy-start | bytes 49156
  5.5 35.2 %copy-start.7 = (f32[16,256]{1,0:T(8,128)S(1)}, f32[16,256]{1,0:T(8,128)}, u32[]{:S(2)}) copy-start(f32[16,256]{1,0:T(8,128)} %constant.62.clone.refs_4_.refs_5_) | copy-start | bytes 49156
  44.7 11.4 %copy-start.8 = (f32[3,512]{1,0:T(4,128)S(1)}, f32[3,512]{1,0:T(4,128)}, u32[]{:S(2)}) copy-start(f32[3,512]{1,0:T(4,128)} %param.22) | copy-start | bytes 18436
  44.7 11.9 %slice-start = ((f32[3,512]{1,0:T(4,128)}), f32[3,1]{1,0:T(4,128)S(1)}, s32[]{:S(2)}) async-start(f32[3,512]{1,0:T(4,128)} %param.22), calls=%async_computation.3 | async-start | bytes 4096 | tf_op jit(solution)/shard_map/jit(_roll_static)/slice | solution.py:560
  44.7 11.9 %copy-start.9 = (f32[4,512]{1,0:T(4,128)S(1)}, f32[4,512]{1,0:T(4,128)}, u32[]{:S(2)}) copy-start(f32[4,512]{1,0:T(4,128)} %constant.58.clone) | copy-start | bytes 24580
  44.7 74.8 %all-to-all-start.2 = ((f32[64,80,128]{2,1,0:T(8,128)}), f32[64,80,128]{2,1,0:T(8,128)S(1)}, u32[]{:S(2)}, u32[]{:S(2)}) async-start(f32[64,80,128]{2,1,0:T(8,128)} %get-tuple-element.18), calls=%async_computation.2 | async-start | bytes 5242880 | tf_op jit(solution)/shard_map/all_to_all | solution.py:536
  61.6 2.7 %collective-permute-start = (f32[32,48,128]{2,1,0:T(8,128)}, f32[32,48,128]{2,1,0:T(8,128)}, u32[]{:S(2)}, u32[]{:S(2)}) collective-permute-start(f32[32,48,128]{2,1,0:T(8,128)} %get-tuple-element.16), channel_id=1, source_target_pairs={{0,8},{8,0},{1,9},{9,1},{2,10},{10,2},{3,11},{11,3},{4,12},{12,4},... | collective-permute-start | bytes 2359304 | tf_op jit(solution)/shard_map/ppermute | solution.py:572
  67.3 58.0 %copy-start = (f32[32,256]{1,0:T(8,128)S(1)}, f32[32,256]{1,0:T(8,128)}, u32[]{:S(2)}) copy-start(f32[32,256]{1,0:T(8,128)} %constant.65.clone.bc_ref) | copy-start | bytes 98308
  67.3 58.0 %copy-start.1 = (f32[32,256]{1,0:T(8,128)S(1)}, f32[32,256]{1,0:T(8,128)}, u32[]{:S(2)}) copy-start(f32[32,256]{1,0:T(8,128)} %constant.66.clone.bs_ref) | copy-start | bytes 98308
  67.3 58.0 %copy-start.4 = (f32[16,256]{1,0:T(8,128)S(1)}, f32[16,256]{1,0:T(8,128)}, u32[]{:S(2)}) copy-start(f32[16,256]{1,0:T(8,128)} %constant.63.clone.ac_ref) | copy-start | bytes 49156
  67.3 58.0 %copy-start.5 = (f32[16,256]{1,0:T(8,128)S(1)}, f32[16,256]{1,0:T(8,128)}, u32[]{:S(2)}) copy-start(f32[16,256]{1,0:T(8,128)} %constant.64.clone.as_ref) | copy-start | bytes 49156
  119.5 48.6 %all-to-all-start.1 = ((f32[32,2,48,128]{3,2,1,0:T(8,128)}), f32[32,2,48,128]{3,2,1,0:T(8,128)}, u32[]{:S(2)}, u32[]{:S(2)}) async-start(f32[32,2,48,128]{3,2,1,0:T(8,128)} %copy.38), calls=%async_computation.1 | async-start | bytes 3145728 | tf_op jit(solution)/shard_map/all_to_all | solution.py:536
  132.7 2.0 %collective-permute-start.1 = (f32[8,128]{1,0:T(8,128)S(1)}, f32[8,128]{1,0:T(8,128)S(1)}, u32[]{:S(2)}, u32[]{:S(2)}) collective-permute-start(f32[8,128]{1,0:T(8,128)S(1)} %get-tuple-element.22), channel_id=1, source_target_pairs={{0,8},{8,0},{1,9},{9,1},{2,10},{10,2},{3,11},{11,3},{4,12},{12,4},... | collective-permute-start | bytes 12296 | tf_op jit(solution)/shard_map/ppermute | solution.py:546
  134.8 3.9 %collective-permute-start.2 = (f32[8,128]{1,0:T(8,128)S(1)}, f32[8,128]{1,0:T(8,128)S(1)}, u32[]{:S(2)}, u32[]{:S(2)}) collective-permute-start(f32[8,128]{1,0:T(8,128)S(1)} %add.53), channel_id=1, source_target_pairs={{0,64},{64,0},{128,192},{192,128},{1,65},{65,1},{129,193},{193,129... | collective-permute-start | bytes 12296 | tf_op jit(solution)/shard_map/ppermute | solution.py:546
  136.2 4.4 %collective-permute-start.3 = (f32[8,128]{1,0:T(8,128)S(1)}, f32[8,128]{1,0:T(8,128)S(1)}, u32[]{:S(2)}, u32[]{:S(2)}) collective-permute-start(f32[8,128]{1,0:T(8,128)S(1)} %add.53), channel_id=1, source_target_pairs={{0,128},{64,192},{128,0},{192,64},{1,129},{65,193},{129,1},{193,65... | collective-permute-start | bytes 12296 | tf_op jit(solution)/shard_map/ppermute | solution.py:546
  138.7 4.1 %collective-permute-start.4 = (f32[8,128]{1,0:T(8,128)S(1)}, f32[8,128]{1,0:T(8,128)S(1)}, u32[]{:S(2)}, u32[]{:S(2)}) collective-permute-start(f32[8,128]{1,0:T(8,128)S(1)} %add.53), channel_id=1, source_target_pairs={{0,192},{64,128},{128,64},{192,0},{1,193},{65,129},{129,65},{193,1... | collective-permute-start | bytes 12296 | tf_op jit(solution)/shard_map/ppermute | solution.py:546
  142.8 3.9 %collective-permute-start.5 = (f32[8,128]{1,0:T(8,128)S(1)}, f32[8,128]{1,0:T(8,128)S(1)}, u32[]{:S(2)}, u32[]{:S(2)}) collective-permute-start(f32[8,128]{1,0:T(8,128)S(1)} %add_add_fusion.2), channel_id=1, source_target_pairs={{0,1},{1,0},{2,3},{3,2},{4,5},{5,4},{6,7},{7,6},{8,9},{9,8},{10,11... | collective-permute-start | bytes 12296 | tf_op jit(solution)/shard_map/ppermute | solution.py:546
  142.8 4.6 %collective-permute-start.6 = (f32[8,128]{1,0:T(8,128)S(1)}, f32[8,128]{1,0:T(8,128)S(1)}, u32[]{:S(2)}, u32[]{:S(2)}) collective-permute-start(f32[8,128]{1,0:T(8,128)S(1)} %add_add_fusion.2), channel_id=1, source_target_pairs={{0,2},{1,3},{2,0},{3,1},{4,6},{5,7},{6,4},{7,5},{8,10},{9,11},{10,... | collective-permute-start | bytes 12296 | tf_op jit(solution)/shard_map/ppermute | solution.py:546
  145.5 4.4 %collective-permute-start.7 = (f32[8,128]{1,0:T(8,128)S(1)}, f32[8,128]{1,0:T(8,128)S(1)}, u32[]{:S(2)}, u32[]{:S(2)}) collective-permute-start(f32[8,128]{1,0:T(8,128)S(1)} %add_add_fusion.2), channel_id=1, source_target_pairs={{0,3},{1,2},{2,1},{3,0},{4,7},{5,6},{6,5},{7,4},{8,11},{9,10},{10,... | collective-permute-start | bytes 12296 | tf_op jit(solution)/shard_map/ppermute | solution.py:546
  149.9 5.7 %collective-permute-start.10 = (f32[8,128]{1,0:T(8,128)S(1)}, f32[8,128]{1,0:T(8,128)S(1)}, u32[]{:S(2)}, u32[]{:S(2)}) collective-permute-start(f32[8,128]{1,0:T(8,128)S(1)} %add_add_fusion.1), channel_id=1, source_target_pairs={{0,48},{16,32},{32,16},{48,0},{1,49},{17,33},{33,17},{49,1},{2,50}... | collective-permute-start | bytes 12296 | tf_op jit(solution)/shard_map/ppermute | solution.py:546
  153.1 3.9 %collective-permute-start.8 = (f32[8,128]{1,0:T(8,128)S(1)}, f32[8,128]{1,0:T(8,128)S(1)}, u32[]{:S(2)}, u32[]{:S(2)}) collective-permute-start(f32[8,128]{1,0:T(8,128)S(1)} %add_add_fusion.1), channel_id=1, source_target_pairs={{0,16},{16,0},{32,48},{48,32},{1,17},{17,1},{33,49},{49,33},{2,18}... | collective-permute-start | bytes 12296 | tf_op jit(solution)/shard_map/ppermute | solution.py:546
  154.8 8.4 %collective-permute-start.9 = (f32[8,128]{1,0:T(8,128)S(1)}, f32[8,128]{1,0:T(8,128)S(1)}, u32[]{:S(2)}, u32[]{:S(2)}) collective-permute-start(f32[8,128]{1,0:T(8,128)S(1)} %add_add_fusion.1), channel_id=1, source_target_pairs={{0,32},{16,48},{32,0},{48,16},{1,33},{17,49},{33,1},{49,17},{2,34}... | collective-permute-start | bytes 12296 | tf_op jit(solution)/shard_map/ppermute | solution.py:546
  163.2 9.7 %collective-permute-start.11 = (f32[8,128]{1,0:T(8,128)S(1)}, f32[8,128]{1,0:T(8,128)S(1)}, u32[]{:S(2)}, u32[]{:S(2)}) collective-permute-start(f32[8,128]{1,0:T(8,128)S(1)} %add_add_fusion), channel_id=1, source_target_pairs={{0,4},{4,0},{1,5},{5,1},{2,6},{6,2},{3,7},{7,3},{8,12},{12,8},{9,1... | collective-permute-start | bytes 12296 | tf_op jit(solution)/shard_map/ppermute | solution.py:546
